TPU v7x, 8 devices: a whole 2x2x1 slice. The times are simulated.
8 devices in a mesh: slab: 1 (over z), coil: 2 (over y), rows: 4 (over x, core).
Axes of the slice: x: 2, y: 2, z: 1, core: 2. Of those that a mesh axis runs over, the one named last changes fastest.
Arguments:
- kspace: float32 [2, 16, 20480], P(None, 'coil', ('slab', 'rows'))
- weight_row: float32 [4, 20480], P(None, ('slab', 'rows'))
- weight_col: float32 [4, 20480], P(None, ('slab', 'rows'))
- grid_row: int32 [20480], P(('slab', 'rows'))
- grid_col: int32 [20480], P(('slab', 'rows'))
- valid_count: int32 [4], P(('slab', 'rows'))
- coil_maps: float32 [2, 16, 320, 320], P(None, 'coil', 'slab', 'rows')
- deapod: float32 [320], replicated
Outputs:
- output: float32 [2, 320, 320], P(None, ('slab', 'coil'), 'rows')
All inputs are finite; a program needn't handle non-finite values.
Results may differ from a plain program's by a relative error of at most 0.001.
Values are sent between devices in bfloat16 or wider.
A program may use at most 1 GiB of HBM per device.

v0:
```python
import math
import jax
import jax.numpy as jnp
from jax import lax
from jax.sharding import PartitionSpec as P


def make_table(n_img):
    n_grid = 2 * n_img
    freq_index = jnp.arange(n_grid, dtype=jnp.int32) - n_img
    pixel_index = jnp.arange(n_img, dtype=jnp.int32) - n_img // 2
    angle_grid = jnp.mod(freq_index[:, None] * pixel_index[None, :], n_grid).astype(jnp.float32) * (2.0 * math.pi / n_grid)
    cos_part = jnp.cos(angle_grid)
    sin_part = jnp.sin(angle_grid)
    return jnp.stack([jnp.stack([cos_part, sin_part], axis=1), jnp.stack([-sin_part, cos_part], axis=1)], axis=0).astype(jnp.bfloat16)


def spread_block(kspace, weight_row, weight_col, grid_row, grid_col, valid_count, first_row, buf_rows, n_grid):
    width = weight_row.shape[0]
    half_width = width // 2
    samples = kspace.shape[2]
    zero_bf = jnp.zeros((), jnp.bfloat16)
    keep_mask = (jnp.arange(samples) < valid_count[0]).astype(jnp.float32)
    row_coef = (kspace[:, :, None, :] * (weight_row * keep_mask)[None, None, :, :]).astype(jnp.bfloat16)
    kernel_idx = jnp.arange(width)
    row_offset = jnp.arange(buf_rows)[:, None] - (grid_row - first_row)[None, :]
    left_side = jnp.sum(jnp.where(row_offset[None, None, None] == kernel_idx[None, None, :, None, None], row_coef[:, :, :, None, :], zero_bf), axis=2)
    col_offset = jnp.mod(jnp.arange(n_grid)[None, :] - grid_col[:, None] + half_width, n_grid)
    right_side = jnp.sum(jnp.where(col_offset[None] == kernel_idx[:, None, None], weight_col.astype(jnp.bfloat16)[:, :, None], zero_bf), axis=0)
    return jnp.einsum('qcrm,mk->qcrk', left_side, right_side, preferred_element_type=jnp.float32)


def solution(mesh):
    n_rows = mesh.shape['rows']
    to_prev = [(index, (index - 1) % n_rows) for index in range(n_rows)]
    to_next = [(index, (index + 1) % n_rows) for index in range(n_rows)]

    def local_part(kspace, weight_row, weight_col, grid_row, grid_col, valid_count, coil_maps, deapod):
        n_img = deapod.shape[0]
        n_grid = 2 * n_img
        block_rows = n_grid // n_rows
        half_width = weight_row.shape[0] // 2
        row_id = lax.axis_index('rows')
        block_grid = spread_block(kspace, weight_row, weight_col, grid_row, grid_col, valid_count, row_id * block_rows, block_rows + 2 * half_width, n_grid)
        from_next = lax.ppermute(block_grid[:, :, :half_width], 'rows', to_prev)
        from_prev = lax.ppermute(block_grid[:, :, block_rows + half_width:], 'rows', to_next)
        own_rows = block_grid[:, :, half_width:half_width + block_rows]
        summed = jnp.concatenate([own_rows[:, :, :half_width] + from_prev, own_rows[:, :, half_width:block_rows - half_width], own_rows[:, :, block_rows - half_width:] + from_next], axis=2).astype(jnp.bfloat16)
        dft_table = make_table(n_img)
        half_image = jnp.einsum('qcrk,qkbj->bcrj', summed, dft_table, preferred_element_type=jnp.float32).astype(jnp.bfloat16)
        columns = lax.all_to_all(half_image, 'rows', 3, 2, tiled=True)
        coil_image = jnp.einsum('bcyj,byei->ecij', columns, dft_table, preferred_element_type=jnp.float32)
        real_part = jnp.sum(coil_maps[0] * coil_image[0] + coil_maps[1] * coil_image[1], axis=0)
        imag_part = jnp.sum(coil_maps[0] * coil_image[1] - coil_maps[1] * coil_image[0], axis=0)
        combined = lax.psum_scatter(jnp.stack([real_part, imag_part]), 'coil', scatter_dimension=1, tiled=True)
        out_rows = combined.shape[1]
        out_cols = combined.shape[2]
        row_scale = lax.dynamic_slice_in_dim(deapod, lax.axis_index('coil') * out_rows, out_rows)
        col_scale = lax.dynamic_slice_in_dim(deapod, row_id * out_cols, out_cols)
        return combined * (row_scale[:, None] * col_scale[None, :])[None]

    spec_samples = P(None, 'coil', ('slab', 'rows'))
    spec_weights = P(None, ('slab', 'rows'))
    spec_index = P(('slab', 'rows'))
    return jax.shard_map(local_part, mesh=mesh, in_specs=(spec_samples, spec_weights, spec_weights, spec_index, spec_index, spec_index, P(None, 'coil', 'slab', 'rows'), P()), out_specs=P(None, ('slab', 'coil'), 'rows'), check_vma=False)
```

profile of v0, /device:TPU:0, one launch (start us, length us, event | category | flops | bytes accessed | tf_op | source)
XLA Modules:
  0.0 194.1 jit_solution(7912444431769900334)
XLA Ops:
  7.2 0.9 convert_element_type.56
  8.1 0.7 broadcast_subtract_fusion
  8.8 0.4 iota_subtract_fusion
  9.2 1.8 iota_compare_fusion.1
  11.0 10.8 %add_select_fusion = s32[5120,640]{1,0:T(8,128)} fusion(s32[5120]{0:T(1024)S(1)} %copy-done.5), kind=kLoop, calls=%fused_computation.4 | loop fusion | flops 26214400 | bytes 13127680 | tf_op jit(solution)/shard_map/jit(remainder)/select_n | solution.py:28
  21.9 0.9 multiply_convert_fusion
  22.8 15.8 %fusion.1 = bf16[5120,640]{1,0:T(8,128)(2,1)} fusion(s32[5120,640]{1,0:T(8,128)} %add_select_fusion, bf16[4,5120]{1,0:T(4,128)(2,1)S(1)} %convert_element_type.56), kind=kLoop, calls=%fused_computation.3 | loop fusion | flops 36044800 | bytes 19701760 | tf_op jit(solution)/shard_map/reduce_sum | solution.py:29
  38.7 50.1 %select_reduce_fusion = bf16[2,8,164,5120]{3,1,2,0:T(8,128)(2,1)} fusion(pred[4,164,5120]{2,1,0:T(8,128)(4,1)S(1)} %iota_compare_fusion.1, bf16[2,8,4,5120]{3,1,2,0:T(8,128)(2,1)} %multiply_convert_fusion), kind=kLoop, calls=%fused_computation | loop fusion | flops 94044160 | bytes 30883840 | tf_op jit(solution)/shard_map/reduce_sum | solution.py:27
  88.8 24.6 %fusion.5 = f32[2,8,164,640]{3,1,2,0:T(8,128)S(1)} fusion(bf16[2,8,164,5120]{3,1,2,0:T(8,128)(2,1)} %select_reduce_fusion, bf16[5120,640]{1,0:T(8,128)(2,1)S(1)} %copy-done), kind=kOutput, calls=%fused_computation.11 | convolution fusion | flops 17196646400 | bytes 40140800 | tf_op jit(solution)/shard_map/qcrm,mk->qcrk/dot_general | solution.py:30
  113.5 2.8 %collective-permute-start.1 = (f32[2,8,2,640]{3,2,1,0:T(2,128)S(1)}, f32[2,8,2,640]{3,2,1,0:T(2,128)S(1)}, u32[]{:S(2)}, u32[]{:S(2)}) collective-permute-start(f32[2,8,2,640]{3,2,1,0:T(2,128)S(1)} %copy.40), channel_id=1, source_target_pairs={{0,3},{1,0},{2,1},{3,2},{4,7},{5,4},{6,5},{7,6}} | collective-permute-start | bytes 245768 | tf_op jit(solution)/shard_map/ppermute | solution.py:45
  116.4 0.3 slice.47
  116.7 0.4 copy.55
  117.1 3.8 %fusion.18 = (bf16[640,1,320]{0,2,1:T(8,128)(2,1)S(1)}, bf16[640,1,320]{0,2,1:T(8,128)(2,1)S(1)}, bf16[640,1,320]{0,2,1:T(8,128)(2,1)S(1)}) fusion(s32[320]{0:T(512)S(1)} %iota_add_fusion.1, s32[640]{0:T(1024)S(1)} %iota_add_fusion), kind=kLoop, calls=%fused_computation.37 | loop fusion | flops 2662400 | bytes 1232640 | tf_op jit(solution)/shard_map/convert.13
  120.9 0.2 maximum_bitcast_fusion.3
  121.1 0.1 fusion.20
  121.3 0.7 copy-done.2
  122.0 5.8 %fusion.10 = bf16[2,8,160,320]{3,2,1,0:T(8,128)(2,1)} fusion(bf16[1,640,2,320]{1,3,0,2:T(8,128)(2,1)S(1)} %get-tuple-element.12, bf16[1,640,2,320]{1,3,0,2:T(8,128)(2,1)S(1)} %get-tuple-element.11, bf16[2,8,2,640]{3,2,1,0:T(2,128)(2,1)S(1)} %fusion.20, bf16[2,8,156,640]{3,2,1,0:T(8,128)(2,1)S(1)} %copy.55, bf16[2,8,2,640]{3,2,1,0:T(2,128)(2,1)S(1)} %fusion.21), kind=kOutput, calls=%fused_computation.20 | convolution fusion | flops 2111078400 | bytes 6553600 | tf_op jit(solution)/shard_map/qcrk,qkbj->bcrj/dot_general | solution.py:50
  127.9 3.9 %copy.25 = bf16[2,8,160,320]{2,1,0,3:T(8,128)(2,1)S(1)} copy(bf16[2,8,160,320]{3,2,1,0:T(8,128)(2,1)} %fusion.10) | data formatting | bytes 3276800 | tf_op jit(solution)/shard_map/convert_element_type | solution.py:50
  131.7 34.1 %all_to_all.18 = bf16[2,8,160,320]{2,1,0,3:T(8,128)(2,1)S(1)} all-to-all(bf16[2,8,160,320]{2,1,0,3:T(8,128)(2,1)S(1)} %copy.25), channel_id=1, replica_groups=mesh['slab'=1,'coil'=2,'rows'=4] {'rows'}, dimensions={3} | all-to-all | bytes 3276800 | tf_op jit(solution)/shard_map/all_to_all | solution.py:51
  165.8 2.0 %copy.56 = bf16[2,8,160,4,80]{2,3,4,0,1:T(4,128)(2,1)S(1)} copy(bf16[2,8,160,4,80]{2,1,0,4,3:T(8,128)(2,1)S(1)} %bitcast.49) | data formatting | bytes 3276800 | tf_op jit(solution)/shard_map/all_to_all | solution.py:51
  167.8 2.8 %reshape.252 = bf16[2,8,640,80,1]{2,3,0,1,4:T(8,128)(2,1)} reshape(bf16[2,8,4,160,80]{3,2,4,0,1:T(4,128)(2,1)S(1)} %bitcast.50) | data formatting | bytes 3276800 | tf_op jit(solution)/shard_map/all_to_all | solution.py:51
  170.6 3.3 %convolution_bitcast_fusion = f32[2,8,320,80]{2,3,1,0:T(8,128)S(1)} fusion(bf16[2,8,640,80,1]{2,3,0,1,4:T(8,128)(2,1)} %reshape.252, bf16[1,640,2,320]{1,3,0,2:T(8,128)(2,1)} %copy-done.2, bf16[1,640,2,320]{1,3,0,2:T(8,128)(2,1)S(1)} %get-tuple-element.11), kind=kOutput, calls=%fused_computation.22 | convolution fusion | flops 1051852800 | bytes 4915200 | tf_op jit(solution)/shard_map/bcyj,byei->ecij/dot_general | solution.py:52
  173.9 0.3 add_reduce_fusion
  174.2 0.2 copy.34
  174.4 0.9 reshape.255
  175.4 0.1 dynamic_slice.7
  175.4 0.1 dynamic_slice.6
  175.5 0.1 broadcast_multiply_fusion.1
  175.6 9.6 %reduce-scatter.4.cloned.1.call-done = f32[160,160]{1,0:T(8,128)} async-done(((f32[320,160]{1,0:T(8,128)}), f32[160,160]{1,0:T(8,128)}) %reduce-scatter.4.cloned.1.call-update) | async-done | bytes 102416
  185.2 1.1 reshape.256
  186.2 0.1 copy.35
  186.4 0.8 copy.27
  (28 shorter events, 0.3 us)
Async XLA Ops:
  6.5 178.6 %reduce-scatter.4.cloned.1.call-start = ((), (), s32[]{:S(2)}) async-start(), calls=%async_computation.2 | async-start | bytes 491520
  9.2 1.8 copy-start.5
  11.0 10.8 %copy-start.4 = (f32[4,5120]{1,0:T(4,128)S(1)}, f32[4,5120]{1,0:T(4,128)}, u32[]{:S(2)}) copy-start(f32[4,5120]{1,0:T(4,128)} %param.9) | copy-start | bytes 245764
  11.0 10.9 %copy-start.3 = (f32[2,8,5120]{2,1,0:T(8,128)S(1)}, f32[2,8,5120]{2,1,0:T(8,128)}, u32[]{:S(2)}) copy-start(f32[2,8,5120]{2,1,0:T(8,128)} %param.8) | copy-start | bytes 983044
  38.7 50.1 %copy-start = (bf16[5120,640]{1,0:T(8,128)(2,1)S(1)}, bf16[5120,640]{1,0:T(8,128)(2,1)}, u32[]{:S(2)}) copy-start(bf16[5120,640]{1,0:T(8,128)(2,1)} %fusion.1) | copy-start | bytes 19660804
  113.5 7.7 %collective-permute-start.1 = (f32[2,8,2,640]{3,2,1,0:T(2,128)S(1)}, f32[2,8,2,640]{3,2,1,0:T(2,128)S(1)}, u32[]{:S(2)}, u32[]{:S(2)}) collective-permute-start(f32[2,8,2,640]{3,2,1,0:T(2,128)S(1)} %copy.40), channel_id=1, source_target_pairs={{0,3},{1,0},{2,1},{3,2},{4,7},{5,4},{6,5},{7,6}} | collective-permute-start | bytes 245768 | tf_op jit(solution)/shard_map/ppermute | solution.py:45
  116.3 4.9 %collective-permute-start = (f32[2,8,2,640]{3,2,1,0:T(2,128)S(1)}, f32[2,8,2,640]{3,2,1,0:T(2,128)S(1)}, u32[]{:S(2)}, u32[]{:S(2)}) collective-permute-start(f32[2,8,2,640]{3,2,1,0:T(2,128)S(1)} %copy.37), channel_id=1, source_target_pairs={{0,1},{1,2},{2,3},{3,0},{4,5},{5,6},{6,7},{7,4}} | collective-permute-start | bytes 245768 | tf_op jit(solution)/shard_map/ppermute | solution.py:46
  121.1 0.9 copy-start.2
  170.6 3.3 %copy-start.1 = (f32[2,8,320,80]{2,3,1,0:T(8,128)S(1)}, f32[2,8,320,80]{2,3,1,0:T(8,128)}, u32[]{:S(2)}) copy-start(f32[2,8,320,80]{2,3,1,0:T(8,128)} %param.14) | copy-start | bytes 4915204
  173.9 1.5 copy-start.6
Sparse Core Ops, SparseCore 0:
  175.5 9.6 reduce-scatter.3
where the time goes:
time: 194 us
  other arithmetic  86 us (44%)
  blocking collectives  34.1 us (18%)
  matrix products  33.7 us (17%)
  between operations  14.3 us (7%)
  local copies, waits for them, and re-layouts  13.5 us (7%)
  waiting for transfers between devices  9.6 us (5%)
  starting transfers between devices  2.83 us (1%)
    reduce_sum x1, other arithmetic, spread_block(): jnp.sum(jnp.where(row_offset[None, None, None] == kernel_idx[None, None,...  50.1 us
    all_to_all x1, blocking collectives, local_part(): columns = lax.all_to_all(half_image, 'rows', 3, 2, tiled=True)  34.1 us
    dot_general x1, matrix products, spread_block(): jnp.einsum('qcrm,mk->qcrk', left_side, right_side, preferred_element_type...  24.6 us
    reduce_sum x1, other arithmetic, spread_block(): jnp.sum(jnp.where(col_offset[None] == kernel_idx[:, None, None], weight_c...  15.8 us
    select_n x1, other arithmetic, spread_block(): jnp.mod(jnp.arange(n_grid)[None, :] - grid_col[:, None] + half_width, n_g...  10.8 us
    unnamed x2, waiting for transfers between devices  9.6 us
    dot_general x1, matrix products, local_part(): jnp.einsum('qcrk,qkbj->bcrj', summed, dft_table, preferred_element_type=j...  5.84 us
    all_to_all x2, local copies, waits for them, and re-layouts, local_part(): columns = lax.all_to_all(half_image, 'rows', 3, 2, tiled=True)  4.78 us
  transfers between devices with their start and end apart: 3, of which 1 were waited for; matrix products, arithmetic and copies ran while one was open for 3% of the time, Pallas kernels for 0%

commit v1 on v0

v1 whole, which is shorter than its diff:
```python
import functools
import numpy as np
import jax
import jax.numpy as jnp
from jax import lax
from jax.experimental import pallas as pl
from jax.experimental.pallas import tpu as pltpu
from jax.sharding import PartitionSpec as P

MESH = pl.DeviceIdType.MESH
BF = jnp.bfloat16
F32 = jnp.float32

N_IMG = 320
N_GRID = 640
ROWS = 4
BLK = 160
COLS = 80
NC = 8
SLOTS = 5120
KC = 1280
NK = SLOTS // KC
LANES = 384
B_FIRST = 64
B_ROWS = 32


def row_order():
    pos = np.arange(128)
    rows = pos + np.where(pos >= B_FIRST, B_ROWS, 0)
    rows[126], rows[16] = 16, 158
    rows[127], rows[32] = 32, 159
    return rows


def constants():
    k = np.arange(N_GRID)
    j = np.arange(N_IMG)
    ang = np.mod((k[:, None] - N_IMG) * (j[None, :] - N_IMG // 2), N_GRID) * (2.0 * np.pi / N_GRID)
    cos_t = np.cos(ang)
    sin_t = np.sin(ang)
    lanes = np.full((LANES,), -1)
    lanes[0:N_IMG] = np.arange(N_IMG)
    used = (lanes >= 0)[None, :]
    src = np.maximum(lanes, 0)
    pick = lambda t: np.where(used, t[:, src], 0.0)
    base = np.arange(ROWS)[:, None] * BLK
    ra = (base + row_order()[None, :]).reshape(-1)
    rb = (base + B_FIRST + np.arange(B_ROWS)[None, :]).reshape(-1)
    bf = jnp.bfloat16
    t3a = np.stack([pick(cos_t)[ra], pick(sin_t)[ra]]).reshape(2, ROWS, 128, LANES).astype(bf)
    t3b = np.stack([pick(cos_t)[rb], pick(sin_t)[rb]]).reshape(2, ROWS * B_ROWS, LANES).astype(bf)
    t2 = np.stack([cos_t.T, sin_t.T]).reshape(2, ROWS, COLS, N_GRID).astype(bf)
    return t2, t3a, t3b


def body(y_h, wr_h, wc_h, gr_h, gc_h, vc, s_h, dd_h, t2_h, t3a_h, t3b_h, out_ref,
         y, wr, wc, gr, gc, s_v, dd, rt0, rt1, rt2, rt3, wd, l0, l1, lh, acc, gb, hbuf, recv,
         hs, hr, hrt, t2, t3a, t3b, ib, ia, img, yrecv, ctmp,
         in_sem, t_sem, s_sem, send_sem, recv_sem, hsend_sem, hrecv_sem, ysend_sem, yrecv_sem):
    rts = (rt0, rt1, rt2, rt3)
    lefts = (l0, l1)
    me = lax.axis_index('rows')
    cid = lax.axis_index('coil')
    nxt = lax.rem(me + 1, ROWS)
    prv = lax.rem(me + ROWS - 1, ROWS)
    other = 1 - cid

    barrier = pltpu.get_barrier_semaphore()
    for d in range(1, ROWS):
        pl.semaphore_signal(barrier, inc=1, device_id={'rows': lax.rem(me + d, ROWS)}, device_id_type=MESH)
    pl.semaphore_signal(barrier, inc=1, device_id={'coil': other}, device_id_type=MESH)

    ins = [pltpu.make_async_copy(a, b, in_sem.at[n]) for n, (a, b) in enumerate(
        ((gr_h, gr), (gc_h, gc), (wr_h, wr), (wc_h, wc), (y_h, y)))]
    for c in ins:
        c.start()
    tabs = [
        pltpu.make_async_copy(t2_h.at[0], t2.at[:, 0, :, 0:N_GRID], t_sem.at[0]),
        pltpu.make_async_copy(t2_h.at[1], t2.at[:, 1, :, 0:N_GRID], t_sem.at[1]),
        pltpu.make_async_copy(t2_h.at[0], t2.at[:, 1, :, N_GRID:], t_sem.at[2]),
        pltpu.make_async_copy(t3b_h.at[0], t3b.at[0, :, 0:LANES], t_sem.at[3]),
        pltpu.make_async_copy(t3b_h.at[1], t3b.at[0, :, LANES:], t_sem.at[4]),
        pltpu.make_async_copy(t3b_h.at[0], t3b.at[1, :, LANES:], t_sem.at[5]),
        pltpu.make_async_copy(t3a_h.at[0], t3a.at[:, 0, :, 0:LANES], t_sem.at[6]),
        pltpu.make_async_copy(t3a_h.at[1], t3a.at[:, 0, :, LANES:], t_sem.at[7]),
        pltpu.make_async_copy(t3a_h.at[0], t3a.at[:, 1, :, LANES:], t_sem.at[8]),
    ]
    for c in tabs:
        c.start()
    big = [pltpu.make_async_copy(s_h, s_v, s_sem.at[0]), pltpu.make_async_copy(dd_h, dd, s_sem.at[1])]
    for c in big:
        c.start()
    for c in ins:
        c.wait()

    def build_wd(k):
        sl = pl.ds(k * KC, KC)
        ids = lax.broadcasted_iota(jnp.int32, (168, 1), 0)
        r = ids + jnp.where((ids >= B_FIRST) & (ids < 128), B_ROWS, 0)
        r = jnp.where(ids >= 128, ids - 128 + B_FIRST, r)
        for a, b in ((126, 16), (127, 32), (16, 158), (32, 159), (160, BLK), (161, -2), (162, -1)):
            r = jnp.where(ids == a, b, r)
        keep = (lax.broadcasted_iota(jnp.int32, (1, KC), 1) + k * KC < vc[0]).astype(F32)
        first = gr[:, sl] - me * BLK
        w = jnp.zeros((168, KC), F32)
        for a in range(4):
            w = jnp.where(r == first + (a - 2), wr[a:a + 1, sl] * keep, w)
        wd[:, sl] = w

    def build_rt(k):
        sl = pl.ds(k * KC, KC)
        col = gc[:, sl]
        for n in range(5):
            ids = lax.broadcasted_iota(jnp.int32, (128, 1), 0) + n * 128
            w = jnp.zeros((128, KC), F32)
            for b in range(4):
                t = col + (b - 2)
                t = jnp.where(t < 0, t + N_GRID, jnp.where(t >= N_GRID, t - N_GRID, t))
                w = jnp.where(ids == t, wc[b:b + 1, sl], w)
            rts[k][n * 128:(n + 1) * 128, :] = w.astype(BF)

    def build_left_b(k):
        sl = pl.ds(k * KC, KC)
        w = wd[128:160, sl]
        for q in range(2):
            for c in range(NC):
                lefts[k % 2][q * 256 + c * 32:q * 256 + c * 32 + 32, :] = (y[q, c:c + 1, sl] * w).astype(BF)

    def build_halo(k):
        sl = pl.ds(k * KC, KC)
        for h in range(3):
            for q in range(2):
                lh[k, h * 16 + q * 8:h * 16 + q * 8 + 8, :] = (y[q, :, sl] * wd[160 + h:161 + h, sl])

    def build_left_a(s, k):
        sl = pl.ds(k * KC, KC)
        w = wd[0:128, sl]
        for q in range(2):
            for c in range(2):
                lefts[k % 2][q * 256 + c * 128:q * 256 + c * 128 + 128, :] = (y[q, pl.ds(2 * s + c, 1), sl] * w).astype(BF)

    def nt(a, b):
        return lax.dot_general(a, b, (((1,), (1,)), ((), ())), preferred_element_type=F32)

    def spread(k):
        for q in range(2):
            cs = slice(q * 256, q * 256 + 256)
            part = nt(rts[k][...], lefts[k % 2][cs, :])
            if k == 0:
                acc[:, cs] = part
            else:
                acc[:, cs] += part

    def exchange(stage):
        return [pltpu.make_async_remote_copy(
            src_ref=hbuf.at[stage, lax.rem(me + d, ROWS)], dst_ref=recv.at[stage, me],
            send_sem=send_sem.at[stage, d - 1], recv_sem=recv_sem.at[stage, 3 - d],
            device_id={'rows': lax.rem(me + d, ROWS)}, device_id_type=MESH) for d in (1, 2, 3)]

    def received(stage):
        return [pltpu.make_async_remote_copy(
            src_ref=hbuf.at[stage, 0], dst_ref=recv.at[stage, lax.rem(me + d, ROWS)],
            send_sem=send_sem.at[stage, d - 1], recv_sem=recv_sem.at[stage, d - 1],
            device_id={'rows': lax.rem(me + d, ROWS)}, device_id_type=MESH) for d in (1, 2, 3)]

    def transform(stage):
        for n in range(ROWS):
            hbuf[stage, n] = jnp.dot(t2[n].reshape(2 * COLS, 2 * N_GRID), gb[...], preferred_element_type=F32).astype(BF)
        for c in exchange(stage):
            c.start()
        recv[stage, me] = hbuf[stage, me]

    build_wd(0)
    build_rt(0)
    build_left_b(0)
    for k in range(NK):
        spread(k)
        if k + 1 < NK:
            build_wd(k + 1)
            build_rt(k + 1)
            build_left_b(k + 1)
    for q in range(2):
        gb[q * N_GRID:(q + 1) * N_GRID, :] = acc[:, q * 256:q * 256 + 256].astype(BF)
    for c in tabs:
        c.wait()
    t2[:, 0, :, N_GRID:] = -t2[:, 1, :, 0:N_GRID]
    t3b[1, :, 0:LANES] = -t3b[0, :, LANES:]
    t3a[:, 1, :, 0:LANES] = -t3a[:, 0, :, LANES:]
    pl.semaphore_wait(barrier, 4)
    transform(0)

    for k in range(NK):
        build_halo(k)
    halo = jnp.zeros((N_GRID, 48), F32)
    for k in range(NK):
        halo = halo + nt(rts[k][...], lh[k].astype(BF))
    hs[...] = halo.T
    to_next = pltpu.make_async_remote_copy(
        src_ref=hs.at[0:16], dst_ref=hr.at[0:16], send_sem=hsend_sem.at[0], recv_sem=hrecv_sem.at[0],
        device_id={'rows': nxt}, device_id_type=MESH)
    to_prev = pltpu.make_async_remote_copy(
        src_ref=hs.at[16:48], dst_ref=hr.at[16:48], send_sem=hsend_sem.at[1], recv_sem=hrecv_sem.at[1],
        device_id={'rows': prv}, device_id_type=MESH)
    to_next.start()
    to_prev.start()
    big[0].wait()
    big[1].wait()
    build_left_a(0, 0)

    def image_first():
        for c in received(0):
            c.wait_recv()
        for c in range(NC):
            lo = (c // 4) * 128
            parts = []
            for b in range(2):
                for p in range(ROWS):
                    parts.append(recv[0, p, b * COLS:(b + 1) * COLS, c * 32:c * 32 + 32])
            lhs = jnp.concatenate(parts, axis=1)
            ib[c] = jnp.dot(lhs, t3b[...].reshape(256, 2 * LANES), preferred_element_type=F32)

    def image_coils(s):
        stage = s + 1
        for c in received(stage):
            c.wait_recv()
        for c in range(2):
            tot = ib[2 * s + c]
            for p in range(ROWS):
                lhs = jnp.concatenate([recv[stage, p, b * COLS:(b + 1) * COLS, c * 128:c * 128 + 128] for b in range(2)], axis=1)
                tot = tot + jnp.dot(lhs, t3a[p].reshape(256, 2 * LANES), preferred_element_type=F32)
            ia[c] = tot
        for c in range(2):
            sr = s_v[0, 2 * s + c]
            si = s_v[1, 2 * s + c]
            re = ia[c, :, 0:N_IMG]
            im = ia[c, :, LANES:LANES + N_IMG]
            img[0, :, 0:N_IMG] += sr * re + si * im
            img[1, :, 0:N_IMG] += sr * im - si * re

    img[...] = jnp.zeros_like(img)

    @pl.loop(0, NC // 2)
    def _(s):
        for k in range(NK):
            spread(k)
            build_left_a(jnp.minimum(s + 1, NC // 2 - 1) if k + 1 == NK else s, (k + 1) % NK)

        @pl.when(s == 0)
        def _():
            to_next.wait()
            to_prev.wait()
            hrt[...] = jnp.concatenate([hr[...], jnp.zeros((80, N_GRID), F32)], axis=0).T

        lane = lax.broadcasted_iota(jnp.int32, (1, 128), 1)
        edge = (lane == 0) | (lane == 16) | (lane == 32)
        for q in range(2):
            for c in range(2):
                rolled = pltpu.roll(hrt[...], 128 - (q * 8 + 2 * s + c), 1)
                cs = slice(q * 256 + c * 128, q * 256 + c * 128 + 128)
                gb[q * N_GRID:(q + 1) * N_GRID, c * 128:c * 128 + 128] = (acc[:, cs] + jnp.where(edge, rolled, 0.0)).astype(BF)
        transform(s + 1)

        @pl.when(s == 0)
        def _():
            image_first()

        @pl.when(s > 0)
        def _():
            image_coils(s - 1)

    image_coils(NC // 2 - 1)

    sends = [pltpu.make_async_remote_copy(
        src_ref=img.at[e, :, pl.ds(pl.multiple_of(other * 128, 128), 256)], dst_ref=yrecv.at[e],
        send_sem=ysend_sem.at[e], recv_sem=yrecv_sem.at[e],
        device_id={'coil': other}, device_id_type=MESH) for e in range(2)]
    for c in sends:
        c.start()
    for c in sends:
        c.wait()
    for e in range(2):
        total = img[e, :, pl.ds(pl.multiple_of(cid * 128, 128), 256)] + yrecv[e]
        ctmp[e] = total.T
        out_ref[e] = ctmp[e, pl.ds(pl.multiple_of(cid * 32, 32), BLK), :] * dd[...]
    for stage in range(5):
        for c in received(stage):
            c.wait_send()


def solution(mesh):
    t2c, t3ac, t3bc = constants()

    def local_part(kspace, weight_row, weight_col, grid_row, grid_col, valid_count, coil_maps, deapod):
        row_scale = lax.dynamic_slice_in_dim(deapod, lax.axis_index('coil') * BLK, BLK)
        col_scale = lax.dynamic_slice_in_dim(deapod, lax.axis_index('rows') * COLS, COLS)
        dd = row_scale[:, None] * col_scale[None, :]
        any_spec = pl.BlockSpec(memory_space=pl.ANY)
        dma = pltpu.SemaphoreType.DMA
        return pl.pallas_call(
            body,
            out_shape=jax.ShapeDtypeStruct((2, BLK, COLS), F32),
            in_specs=[any_spec] * 5 + [pl.BlockSpec(memory_space=pltpu.SMEM)] + [any_spec] * 5,
            out_specs=pl.BlockSpec(memory_space=pltpu.VMEM),
            scratch_shapes=[
                pltpu.VMEM((2, NC, SLOTS), F32),
                pltpu.VMEM((4, SLOTS), F32),
                pltpu.VMEM((4, SLOTS), F32),
                pltpu.VMEM((1, SLOTS), jnp.int32),
                pltpu.VMEM((1, SLOTS), jnp.int32),
                pltpu.VMEM((2, NC, COLS, N_IMG), F32),
                pltpu.VMEM((BLK, COLS), F32),
            ] + [pltpu.VMEM((N_GRID, KC), BF)] * 4 + [
                pltpu.VMEM((168, SLOTS), F32),
                pltpu.VMEM((512, KC), BF),
                pltpu.VMEM((512, KC), BF),
                pltpu.VMEM((NK, 48, KC), F32),
                pltpu.VMEM((N_GRID, 512), F32),
                pltpu.VMEM((2 * N_GRID, 256), BF),
                pltpu.VMEM((5, ROWS, 2 * COLS, 256), BF),
                pltpu.VMEM((5, ROWS, 2 * COLS, 256), BF),
                pltpu.VMEM((48, N_GRID), F32),
                pltpu.VMEM((48, N_GRID), F32),
                pltpu.VMEM((N_GRID, 128), F32),
                pltpu.VMEM((ROWS, 2, COLS, 2 * N_GRID), BF),
                pltpu.VMEM((ROWS, 2, 128, 2 * LANES), BF),
                pltpu.VMEM((2, ROWS * B_ROWS, 2 * LANES), BF),
                pltpu.VMEM((NC, COLS, 2 * LANES), F32),
                pltpu.VMEM((2, COLS, 2 * LANES), F32),
                pltpu.VMEM((2, COLS, LANES), F32),
                pltpu.VMEM((2, COLS, 256), F32),
                pltpu.VMEM((2, 256, COLS), F32),
                dma((5,)), dma((9,)), dma((2,)), dma((5, 3)), dma((5, 3)), dma((2,)), dma((2,)), dma((2,)), dma((2,)),
            ],
            compiler_params=pltpu.CompilerParams(collective_id=0, has_side_effects=True, vmem_limit_bytes=60 * 1024 * 1024),
            name='nufft_adjoint',
        )(kspace, weight_row, weight_col, grid_row.reshape(1, SLOTS), grid_col.reshape(1, SLOTS), valid_count,
          jnp.swapaxes(coil_maps, 2, 3), dd, jnp.asarray(t2c), jnp.asarray(t3ac), jnp.asarray(t3bc))

    spec_samples = P(None, 'coil', ('slab', 'rows'))
    spec_weights = P(None, ('slab', 'rows'))
    spec_index = P(('slab', 'rows'))
    return jax.shard_map(local_part, mesh=mesh, in_specs=(spec_samples, spec_weights, spec_weights, spec_index, spec_index, spec_index, P(None, 'coil', 'slab', 'rows'), P()), out_specs=P(None, ('slab', 'coil'), 'rows'), check_vma=False)
```

time: 194 us -> 55.6 us (0.29)
  other arithmetic: 86 us -> 0.73 us
  Pallas kernels: 0 us -> 50.9 us
  blocking collectives: 34.1 us -> 0 us
  matrix products: 33.7 us -> 0 us
  between operations: 14.3 us -> 0.66 us
  local copies, waits for them, and re-layouts: 13.5 us -> 3.11 us
  waiting for transfers between devices: 9.6 us -> 0 us
  starting transfers between devices: 2.83 us -> 0 us
    reduce_sum x3 -> x0, other arithmetic: 66.2 us -> none  [the longest x1 50.1 us: spread_block(): jnp.sum(jnp.where(row_offset[None, None, None] == kernel_idx[None, None,...]
    pallas_call x0 -> x1, Pallas kernels: none -> 50.9 us  [local_part(): pl.pallas_call(body, out_shape=jax.ShapeDtypeStruct((2, BLK, COLS), F32),...]
    all_to_all x1 -> x0, blocking collectives: 34.1 us -> none  [local_part(): columns = lax.all_to_all(half_image, 'rows', 3, 2, tiled=True)]
    dot_general x3 -> x0, matrix products: 33.7 us -> none  [the longest x1 24.6 us: spread_block(): jnp.einsum('qcrm,mk->qcrk', left_side, right_side, preferred_element_type...]
    select_n x1 -> x0, other arithmetic: 10.8 us -> none  [spread_block(): jnp.mod(jnp.arange(n_grid)[None, :] - grid_col[:, None] + half_width, n_g...]
    unnamed x2 -> x0, waiting for transfers between devices: 9.6 us -> none
    all_to_all x2 -> x0, local copies, waits for them, and re-layouts: 4.78 us -> none  [local_part(): columns = lax.all_to_all(half_image, 'rows', 3, 2, tiled=True)]
    another operation x5 -> x0, other arithmetic: 4.11 us -> none
  transfers between devices with their start and end apart: 3 -> 0, of which waited for: 1 -> 0; matrix products, arithmetic and copies ran while one was open for 3% -> 0% of each run, Pallas kernels for 0% -> 0%
where the time goes in v1:
time: 55.6 us; the launch traced here: 55.4 us
  Pallas kernels  50.9 us (92%)
  local copies, waits for them, and re-layouts  3.11 us (6%)
  other arithmetic  0.73 us (1%)
  between operations  0.66 us (1%)
    pallas_call x1, Pallas kernels, local_part(): pl.pallas_call(body, out_shape=jax.ShapeDtypeStruct((2, BLK, COLS), F32),...  50.9 us
    unnamed x1, local copies, waits for them, and re-layouts  1.59 us

profile of v1, /device:TPU:0, one launch (start us, length us, event | category | flops | bytes accessed | tf_op | source)
XLA Modules:
  0.0 55.4 jit_solution(13283437471216182403)
XLA Ops:
  0.7 0.8 %dynamic_slice.7 = f32[80]{0:T(128)S(1)} dynamic-slice(f32[320]{0:T(512)} %param.18, s32[]{:T(128)S(6)} %select_n.7), dynamic_slice_sizes={80} | dynamic-slice | bytes 644 | tf_op jit(solution)/shard_map/dynamic_slice | solution.py:296
  1.4 0.8 %dynamic_slice.6 = f32[160]{0:T(256)S(1)} dynamic-slice(f32[320]{0:T(512)} %param.18, s32[]{:T(128)S(6)} %select_n.6), dynamic_slice_sizes={160} | dynamic-slice | bytes 1284 | tf_op jit(solution)/shard_map/dynamic_slice | solution.py:295
  2.2 0.7 %broadcast_multiply_fusion.dd_h = f32[160,80]{1,0:T(8,128)} fusion(f32[80]{0:T(128)S(1)} %dynamic_slice.7, f32[160]{0:T(256)S(1)} %dynamic_slice.6), kind=kLoop, calls=%fused_computation | loop fusion | flops 12800 | bytes 52160 | tf_op jit(solution)/shard_map/mul | solution.py:297
  2.9 50.9 %nufft_adjoint.1 = f32[2,160,80]{2,1,0:T(8,128)} custom-call(f32[2,8,5120]{2,1,0:T(8,128)} %y_h.1, f32[4,5120]{1,0:T(4,128)} %wr_h.1, f32[4,5120]{1,0:T(4,128)} %wc_h.1, s32[1,5120]{1,0:T(1,128)} %bitcast.4, s32[1,5120]{1,0:T(1,128)} %bitcast.5, s32[1]{0:T(128)S(6)} %copy.13.vc, f32[2,8,80,320]{3,2,1,0:T(8,128)} %bitcast.3, ...), custom_call_target="tpu_custom_call" | custom-call | tf_op jit(solution)/shard_map/nufft_adjoint/pallas_call | solution.py:300
  53.8 1.6 %copy.14 = f32[2,160,80]{2,1,0:T(8,128)} copy(f32[2,160,80]{2,1,0:T(8,128)} %nufft_adjoint.1) | data formatting | bytes 204800

commit v2 on v1

v2 whole, which is shorter than its diff:
```python
import functools
import numpy as np
import jax
import jax.numpy as jnp
from jax import lax
from jax.experimental import pallas as pl
from jax.experimental.pallas import tpu as pltpu
from jax.sharding import PartitionSpec as P

MESH = pl.DeviceIdType.MESH
BF = jnp.bfloat16
F32 = jnp.float32

N_IMG = 320
N_GRID = 640
ROWS = 4
BLK = 160
COLS = 80
NC = 8
SLOTS = 5120
KC = 1280
NK = SLOTS // KC
LANES = 384
B_FIRST = 64
B_ROWS = 32


def row_order():
    pos = np.arange(128)
    rows = pos + np.where(pos >= B_FIRST, B_ROWS, 0)
    rows[126], rows[16] = 16, 158
    rows[127], rows[32] = 32, 159
    return rows


def constants():
    k = np.arange(N_GRID)
    j = np.arange(N_IMG)
    ang = np.mod((k[:, None] - N_IMG) * (j[None, :] - N_IMG // 2), N_GRID) * (2.0 * np.pi / N_GRID)
    cos_t = np.cos(ang)
    sin_t = np.sin(ang)
    lanes = np.full((LANES,), -1)
    lanes[0:N_IMG] = np.arange(N_IMG)
    used = (lanes >= 0)[None, :]
    src = np.maximum(lanes, 0)
    pick = lambda t: np.where(used, t[:, src], 0.0)
    base = np.arange(ROWS)[:, None] * BLK
    ra = (base + row_order()[None, :]).reshape(-1)
    rb = (base + B_FIRST + np.arange(B_ROWS)[None, :]).reshape(-1)
    bf = jnp.bfloat16
    t3a = np.stack([pick(cos_t)[ra], pick(sin_t)[ra]]).reshape(2, ROWS, 128, LANES).astype(bf)
    t3b = np.stack([pick(cos_t)[rb], pick(sin_t)[rb]]).reshape(2, ROWS * B_ROWS, LANES).astype(bf)
    t2 = np.stack([cos_t.T, sin_t.T]).reshape(2, ROWS, COLS, N_GRID).astype(bf)
    return t2, t3a, t3b


def body(y_h, wr_h, wc_h, gr_h, gc_h, vc, s_h, d_h, t2_h, t3a_h, t3b_h, out_ref,
         y, wr, wc, gr, gc, s_v, din, drow, dcol, dd, rt0, rt1, rt2, rt3, wd, l0, l1, lh, acc, gb, hbuf, recv,
         hs, hr, hrt, t2, t3a, t3b, ib, img, yrecv, ctmp,
         in_sem, t2_sem, t3_sem, s_sem, send_sem, recv_sem, hsend_sem, hrecv_sem, ysend_sem, yrecv_sem):
    rts = (rt0, rt1, rt2, rt3)
    lefts = (l0, l1)
    me = lax.axis_index('rows')
    cid = lax.axis_index('coil')
    nxt = lax.rem(me + 1, ROWS)
    prv = lax.rem(me + ROWS - 1, ROWS)
    other = 1 - cid

    ins = [pltpu.make_async_copy(a, b, in_sem.at[n]) for n, (a, b) in enumerate(
        ((gc_h, gc), (wc_h, wc), (gr_h, gr), (wr_h, wr), (y_h.at[0], y.at[0:8]), (y_h.at[1], y.at[8:16])))]
    for c in ins:
        c.start()
    tab2 = [
        pltpu.make_async_copy(t2_h.at[0], t2.at[:, 0, :, 0:N_GRID], t2_sem.at[0]),
        pltpu.make_async_copy(t2_h.at[1], t2.at[:, 1, :, 0:N_GRID], t2_sem.at[1]),
        pltpu.make_async_copy(t2_h.at[0], t2.at[:, 1, :, N_GRID:], t2_sem.at[2]),
    ]
    tab3 = []
    for g in range(3):
        src = slice(g * 128, g * 128 + 128)
        re = slice(g * 256, g * 256 + 128)
        im = slice(g * 256 + 128, g * 256 + 256)
        tab3 += [
            (t3b_h.at[0, :, src], t3b.at[0, :, re]),
            (t3b_h.at[1, :, src], t3b.at[0, :, im]),
            (t3b_h.at[0, :, src], t3b.at[1, :, im]),
            (t3a_h.at[0, :, :, src], t3a.at[:, 0, :, re]),
            (t3a_h.at[1, :, :, src], t3a.at[:, 0, :, im]),
            (t3a_h.at[0, :, :, src], t3a.at[:, 1, :, im]),
        ]
    tab3 = [pltpu.make_async_copy(a, b, t3_sem.at[n]) for n, (a, b) in enumerate(tab3)]
    big = [pltpu.make_async_copy(s_h, s_v, s_sem.at[0]),
           pltpu.make_async_copy(d_h, din, s_sem.at[1])]
    for c in tab2 + tab3 + big:
        c.start()

    barrier = pltpu.get_barrier_semaphore()
    for d in range(1, ROWS):
        pl.semaphore_signal(barrier, inc=1, device_id={'rows': lax.rem(me + d, ROWS)}, device_id_type=MESH)
    pl.semaphore_signal(barrier, inc=1, device_id={'coil': other}, device_id_type=MESH)
    for c in ins:
        c.wait()

    pieces = [(k * KC + o, 256) for k in range(NK) for o in range(0, KC, 256)]

    def build_wd(lo, groups):
        sl = pl.ds(lo, 256)
        keep = (lax.broadcasted_iota(jnp.int32, (1, 256), 1) + lo < vc[0]).astype(F32)
        first = gr[:, sl] - me * BLK
        taps = [(jnp.broadcast_to(first + (a - 2), (8, 256)), jnp.broadcast_to(wr[a:a + 1, sl] * keep, (8, 256)))
                for a in range(4)]
        ids = lax.broadcasted_iota(jnp.int32, (8, 1), 0)
        for n in groups:
            if n < 16:
                r = ids + (n * 8 + (B_ROWS if n * 8 >= B_FIRST else 0))
            elif n < 20:
                r = ids + (n * 8 - 128 + B_FIRST)
            else:
                r = jnp.where(ids == 0, BLK, ids - 3)
            for p, v in ((126, 16), (127, 32), (16, 158), (32, 159)):
                if p // 8 == n:
                    r = jnp.where(ids == p % 8, v, r)
            w = jnp.zeros((8, 256), F32)
            for t, v in taps:
                w = jnp.where(r == t, v, w)
            wd[n * 8:n * 8 + 8, sl] = w

    def build_rt(k, off):
        sl = pl.ds(k * KC + off, 256)
        col = gc[:, sl]
        taps = []
        for b in range(4):
            t = col + (b - 2)
            t = jnp.where(t < 0, t + N_GRID, jnp.where(t >= N_GRID, t - N_GRID, t))
            taps.append((jnp.broadcast_to(t, (16, 256)).astype(jnp.int16),
                         jnp.broadcast_to(wc[b:b + 1, sl], (16, 256)).astype(BF)))
        base = lax.broadcasted_iota(jnp.int16, (16, 256), 0)
        for n in range(N_GRID // 16):
            ids = base + jnp.int16(n * 16)
            w = jnp.zeros((16, 256), BF)
            for t, v in taps:
                w = jnp.where(ids == t, v, w)
            rts[k][n * 16:(n + 1) * 16, off:off + 256] = w

    def build_left_b(k, off):
        sl = pl.ds(k * KC + off, 256)
        w = wd[128:160, sl]
        for q in range(2):
            for c in range(NC):
                lo = q * 256 + c * 32
                lefts[k % 2][lo:lo + 32, off:off + 256] = (y[q * 8 + c:q * 8 + c + 1, sl] * w).astype(BF)

    def build_halo(lo):
        sl = pl.ds(lo, 256)
        for h in range(3):
            lh[h * 16:h * 16 + 16, sl] = (y[:, sl] * wd[160 + h:161 + h, sl]).astype(BF)

    def build_left_a(s, k):
        for off in range(0, KC, 256):
            sl = pl.ds(k * KC + off, 256)
            rows = [jnp.broadcast_to(y[pl.ds(q * 8 + 2 * s + c, 1), sl], (16, 256)) for q in range(2) for c in range(2)]
            for n in range(8):
                w = wd[n * 16:n * 16 + 16, sl]
                for m, row in enumerate(rows):
                    lefts[k % 2][m * 128 + n * 16:m * 128 + n * 16 + 16, off:off + 256] = (row * w).astype(BF)

    def nt(a, b):
        return lax.dot_general(a, b, (((1,), (1,)), ((), ())), preferred_element_type=F32)

    def exchange(stage):
        return [pltpu.make_async_remote_copy(
            src_ref=hbuf.at[stage, lax.rem(me + d, ROWS)], dst_ref=recv.at[stage, me],
            send_sem=send_sem.at[stage, d - 1], recv_sem=recv_sem.at[stage, 3 - d],
            device_id={'rows': lax.rem(me + d, ROWS)}, device_id_type=MESH) for d in (1, 2, 3)]

    def received(stage):
        return [pltpu.make_async_remote_copy(
            src_ref=hbuf.at[stage, 0], dst_ref=recv.at[stage, lax.rem(me + d, ROWS)],
            send_sem=send_sem.at[stage, d - 1], recv_sem=recv_sem.at[stage, d - 1],
            device_id={'rows': lax.rem(me + d, ROWS)}, device_id_type=MESH) for d in (1, 2, 3)]

    def transform(stage):
        for n in range(ROWS):
            hbuf[stage, n] = jnp.dot(t2[n].reshape(2 * COLS, 2 * N_GRID), gb[...], preferred_element_type=F32).astype(BF)
        for c in exchange(stage):
            c.start()
        recv[stage, me] = hbuf[stage, me]

    parts = [(0, 0, 256), (0, 256, KC - 256)] + [(k, 0, KC) for k in range(1, NK)]

    def build_first(k, off, size):
        for o in range(off, off + size, 256):
            build_rt(k, o)
            build_wd(k * KC + o, (16, 17, 18, 19, 20))
            build_left_b(k, o)

    build_first(*parts[0])
    for n, (k, off, size) in enumerate(parts):
        for q in range(2):
            cs = slice(q * 256, q * 256 + 256)
            part = nt(rts[k][:, off:off + size], lefts[k % 2][cs, off:off + size])
            if n == 0:
                acc[:, cs] = part
            elif n + 1 < len(parts):
                acc[:, cs] += part
            else:
                gb[q * N_GRID:(q + 1) * N_GRID, :] = (acc[:, cs] + part).astype(BF)
        if n + 1 < len(parts):
            build_first(*parts[n + 1])
    for c in tab2:
        c.wait()
    t2[:, 0, :, N_GRID:] = -t2[:, 1, :, 0:N_GRID]
    pl.semaphore_wait(barrier, 4)
    transform(0)

    for c in tab3 + big:
        c.wait()
    for lo, _ in pieces:
        build_halo(lo)
    for h in range(2):
        rows = slice(h * 320, h * 320 + 320)
        halo = nt(rts[0][rows, :], lh[:, 0:KC])
        for k in range(1, NK):
            halo = halo + nt(rts[k][rows, :], lh[:, k * KC:(k + 1) * KC])
        hrt[rows, 0:48] = halo
    for lo, _ in pieces:
        build_wd(lo, range(16))
    for g in range(3):
        lanes = slice(g * 256, g * 256 + 128)
        t3b[1, :, lanes] = -t3b[0, :, g * 256 + 128:g * 256 + 256]
        t3a[:, 1, :, lanes] = -t3a[:, 0, :, g * 256 + 128:g * 256 + 256]
    drow[:, 0:N_IMG] = din[...].reshape(1, N_IMG)
    dcol[...] = jnp.broadcast_to(din[...].reshape(1, N_IMG), (8, N_IMG)).T
    dd[...] = dcol[pl.ds(pl.multiple_of(me * COLS, COLS), COLS), 0:1] * drow[:, pl.ds(pl.multiple_of(cid * 128, 128), 256)]
    img[...] = jnp.zeros_like(img)
    hs[...] = hrt[...].T[0:48]
    build_left_a(0, 0)
    to_next = pltpu.make_async_remote_copy(
        src_ref=hs.at[0:16], dst_ref=hr.at[0:16], send_sem=hsend_sem.at[0], recv_sem=hrecv_sem.at[0],
        device_id={'rows': nxt}, device_id_type=MESH)
    to_prev = pltpu.make_async_remote_copy(
        src_ref=hs.at[16:48], dst_ref=hr.at[16:48], send_sem=hsend_sem.at[1], recv_sem=hrecv_sem.at[1],
        device_id={'rows': prv}, device_id_type=MESH)
    to_next.start()
    to_prev.start()

    def image_first():
        for c in received(0):
            c.wait_recv()
        for c in range(NC):
            blocks = [recv[0, p, b * COLS:(b + 1) * COLS, c * 32:c * 32 + 32] for b in range(2) for p in range(ROWS)]
            lhs = jnp.concatenate(blocks, axis=1)
            ib[c // 2, (c % 2) * COLS:(c % 2 + 1) * COLS] = jnp.dot(lhs, t3b[...].reshape(256, 2 * LANES), preferred_element_type=F32)

    def image_coils(s):
        stage = s + 1
        for c in received(stage):
            c.wait_recv()
        lhs = jnp.concatenate([jnp.concatenate(
            [recv[stage, p, b * COLS:(b + 1) * COLS, c * 128:c * 128 + 128] for p in range(ROWS) for b in range(2)], axis=1)
            for c in range(2)], axis=0)
        for g in range(3):
            lanes = slice(g * 256, g * 256 + 256)
            tot = ib[s, :, lanes] + jnp.dot(lhs, t3a[:, :, :, lanes].reshape(1024, 256), preferred_element_type=F32)
            n = min(128, N_IMG - g * 128)
            at = slice(g * 128, g * 128 + n)
            add_re = img[0, :, at]
            add_im = img[1, :, at]
            for c in range(2):
                sr = s_v[0, 2 * s + c, :, at]
                si = s_v[1, 2 * s + c, :, at]
                re = tot[c * COLS:(c + 1) * COLS, 0:n]
                im = tot[c * COLS:(c + 1) * COLS, 128:128 + n]
                add_re = add_re + (sr * re + si * im)
                add_im = add_im + (sr * im - si * re)
            img[0, :, at] = add_re
            img[1, :, at] = add_im

    @pl.loop(0, NC // 2)
    def _(s):
        for k in range(NK - 1):
            for q in range(2):
                cs = slice(q * 256, q * 256 + 256)
                part = nt(rts[k][...], lefts[k % 2][cs, :])
                if k == 0:
                    acc[:, cs] = part
                else:
                    acc[:, cs] += part
            build_left_a(s, k + 1)

        @pl.when(s == 0)
        def _():
            to_next.wait()
            to_prev.wait()
            hrt[...] = jnp.concatenate([hr[...], jnp.zeros((80, N_GRID), F32)], axis=0).T

        k = NK - 1
        lane = lax.broadcasted_iota(jnp.int32, (1, 128), 1)
        edge = (lane == 0) | (lane == 16) | (lane == 32)
        for q in range(2):
            part = nt(rts[k][...], lefts[k % 2][q * 256:q * 256 + 256, :])
            for c in range(2):
                rolled = pltpu.roll(hrt[...], 128 - (q * 8 + 2 * s + c), 1)
                lo = q * 256 + c * 128
                whole = acc[:, lo:lo + 128] + part[:, c * 128:c * 128 + 128] + jnp.where(edge, rolled, 0.0)
                gb[q * N_GRID:(q + 1) * N_GRID, c * 128:c * 128 + 128] = whole.astype(BF)
        build_left_a(jnp.minimum(s + 1, NC // 2 - 1), 0)
        transform(s + 1)

        @pl.when(s == 0)
        def _():
            image_first()

        @pl.when(s > 0)
        def _():
            image_coils(s - 1)

    image_coils(NC // 2 - 1)

    sends = [pltpu.make_async_remote_copy(
        src_ref=img.at[e, :, pl.ds(pl.multiple_of(other * 128, 128), 256)], dst_ref=yrecv.at[e],
        send_sem=ysend_sem.at[e], recv_sem=yrecv_sem.at[e],
        device_id={'coil': other}, device_id_type=MESH) for e in range(2)]
    for c in sends:
        c.start()
    for e in range(2):
        sends[e].wait()
        total = (img[e, :, pl.ds(pl.multiple_of(cid * 128, 128), 256)] + yrecv[e]) * dd[...]
        ctmp[e] = total.T
        out_ref[e] = ctmp[e, pl.ds(pl.multiple_of(cid * 32, 32), BLK), :]
    for stage in range(5):
        for c in received(stage):
            c.wait_send()


def solution(mesh):
    t2c, t3ac, t3bc = constants()

    def local_part(kspace, weight_row, weight_col, grid_row, grid_col, valid_count, coil_maps, deapod):
        any_spec = pl.BlockSpec(memory_space=pl.ANY)
        dma = pltpu.SemaphoreType.DMA
        return pl.pallas_call(
            body,
            out_shape=pltpu.VMEM((2, BLK, COLS), F32),
            in_specs=[any_spec] * 5 + [pl.BlockSpec(memory_space=pltpu.SMEM)] + [any_spec] * 5,
            out_specs=pl.BlockSpec(memory_space=pltpu.VMEM),
            scratch_shapes=[
                pltpu.VMEM((2 * NC, SLOTS), F32),
                pltpu.VMEM((4, SLOTS), F32),
                pltpu.VMEM((4, SLOTS), F32),
                pltpu.VMEM((1, SLOTS), jnp.int32),
                pltpu.VMEM((1, SLOTS), jnp.int32),
                pltpu.VMEM((2, NC, COLS, N_IMG), F32),
                pltpu.VMEM((N_IMG,), F32),
                pltpu.VMEM((1, LANES), F32),
                pltpu.VMEM((N_IMG, 8), F32),
                pltpu.VMEM((COLS, 256), F32),
            ] + [pltpu.VMEM((N_GRID, KC), BF)] * 4 + [
                pltpu.VMEM((168, SLOTS), F32),
                pltpu.VMEM((512, KC), BF),
                pltpu.VMEM((512, KC), BF),
                pltpu.VMEM((48, SLOTS), BF),
                pltpu.VMEM((N_GRID, 512), F32),
                pltpu.VMEM((2 * N_GRID, 256), BF),
                pltpu.VMEM((5, ROWS, 2 * COLS, 256), BF),
                pltpu.VMEM((5, ROWS, 2 * COLS, 256), BF),
                pltpu.VMEM((48, N_GRID), F32),
                pltpu.VMEM((48, N_GRID), F32),
                pltpu.VMEM((N_GRID, 128), F32),
                pltpu.VMEM((ROWS, 2, COLS, 2 * N_GRID), BF),
                pltpu.VMEM((ROWS, 2, 128, 2 * LANES), BF),
                pltpu.VMEM((2, ROWS * B_ROWS, 2 * LANES), BF),
                pltpu.VMEM((NC // 2, 2 * COLS, 2 * LANES), F32),
                pltpu.VMEM((2, COLS, LANES), F32),
                pltpu.VMEM((2, COLS, 256), F32),
                pltpu.VMEM((2, 256, COLS), F32),
                dma((6,)), dma((3,)), dma((18,)), dma((2,)), dma((5, 3)), dma((5, 3)), dma((2,)), dma((2,)), dma((2,)), dma((2,)),
            ],
            compiler_params=pltpu.CompilerParams(collective_id=0, has_side_effects=True, vmem_limit_bytes=60 * 1024 * 1024),
            name='nufft_adjoint',
        )(kspace, weight_row, weight_col, grid_row.reshape(1, SLOTS), grid_col.reshape(1, SLOTS), valid_count,
          jnp.swapaxes(coil_maps, 2, 3), deapod, jnp.asarray(t2c), jnp.asarray(t3ac), jnp.asarray(t3bc))

    spec_samples = P(None, 'coil', ('slab', 'rows'))
    spec_weights = P(None, ('slab', 'rows'))
    spec_index = P(('slab', 'rows'))
    return jax.shard_map(local_part, mesh=mesh, in_specs=(spec_samples, spec_weights, spec_weights, spec_index, spec_index, spec_index, P(None, 'coil', 'slab', 'rows'), P()), out_specs=P(None, ('slab', 'coil'), 'rows'), check_vma=False)
```

time: 55.6 us -> 43.9 us (0.79)
  Pallas kernels: 50.9 us -> 42.4 us
  local copies, waits for them, and re-layouts: 3.11 us -> 0.67 us
  other arithmetic: 0.73 us -> 0 us
    pallas_call x1, Pallas kernels: 50.9 us -> 42.4 us  [local_part(): pl.pallas_call(body, out_shape=pltpu.VMEM((2, BLK, COLS), F32), in_specs=...]
    dynamic_slice x2 -> x0, local copies, waits for them, and re-layouts: 1.51 us -> none  [the longest x1 0.76 us: local_part(): lax.dynamic_slice_in_dim(deapod, lax.axis_index('rows') * COLS, COLS)]
    unnamed x1, local copies, waits for them, and re-layouts: 1.59 us -> 0.67 us
    mul x1 -> x0, other arithmetic: 0.73 us -> none  [local_part(): dd = row_scale[:, None] * col_scale[None, :]]
where the time goes in v2:
time: 43.9 us; the launch traced here: 43.8 us
  Pallas kernels  42.4 us (97%)
  local copies, waits for them, and re-layouts  0.67 us (2%)
  between operations  0.66 us (2%)
    pallas_call x1, Pallas kernels, local_part(): pl.pallas_call(body, out_shape=pltpu.VMEM((2, BLK, COLS), F32), in_specs=...  42.4 us

profile of v2, /device:TPU:0, one launch (start us, length us, event | category | flops | bytes accessed | tf_op | source)
XLA Modules:
  0.0 43.8 jit_solution(7728619385488936138)
XLA Ops:
  0.7 42.4 %nufft_adjoint.1 = f32[2,160,80]{2,1,0:T(8,128)S(1)} custom-call(f32[2,8,5120]{2,1,0:T(8,128)} %y_h.1, f32[4,5120]{1,0:T(4,128)} %wr_h.1, f32[4,5120]{1,0:T(4,128)} %wc_h.1, s32[1,5120]{1,0:T(1,128)} %bitcast.4, s32[1,5120]{1,0:T(1,128)} %bitcast.5, s32[1]{0:T(128)S(6)} %copy.14.vc, f32[2,8,80,320]{3,2,1,0:T(8,128)} %bitcast.3, f32[320]{0:T(512)} %d_h.1, ...), custom_call_target="tpu_custom_call" | custom-call | tf_op jit(solution)/shard_map/nufft_adjoint/pallas_call | solution.py:342
  43.1 0.7 %copy.13 = f32[2,160,80]{2,1,0:T(8,128)} copy(f32[2,160,80]{2,1,0:T(8,128)S(1)} %nufft_adjoint.1) | data formatting | bytes 204800

commit v3 on v2

v3 whole, which is shorter than its diff:
```python
import functools
import numpy as np
import jax
import jax.numpy as jnp
from jax import lax
from jax.experimental import pallas as pl
from jax.experimental.pallas import tpu as pltpu
from jax.sharding import PartitionSpec as P

MESH = pl.DeviceIdType.MESH
BF = jnp.bfloat16
F32 = jnp.float32

N_IMG = 320
N_GRID = 640
ROWS = 4
BLK = 160
COLS = 80
NC = 8
SLOTS = 5120
KC = 1280
NK = SLOTS // KC
LANES = 384
HALF = SLOTS // 2
LAG = 3
B_FIRST = 64
B_ROWS = 32


def row_order():
    pos = np.arange(128)
    rows = pos + np.where(pos >= B_FIRST, B_ROWS, 0)
    rows[126], rows[16] = 16, 158
    rows[127], rows[32] = 32, 159
    return rows


def constants():
    k = np.arange(N_GRID)
    j = np.arange(N_IMG)
    ang = np.mod((k[:, None] - N_IMG) * (j[None, :] - N_IMG // 2), N_GRID) * (2.0 * np.pi / N_GRID)
    cos_t = np.cos(ang)
    sin_t = np.sin(ang)
    lanes = np.full((LANES,), -1)
    lanes[0:N_IMG] = np.arange(N_IMG)
    used = (lanes >= 0)[None, :]
    src = np.maximum(lanes, 0)
    pick = lambda t: np.where(used, t[:, src], 0.0)
    base = np.arange(ROWS)[:, None] * BLK
    ra = (base + row_order()[None, :]).reshape(-1)
    rb = (base + B_FIRST + np.arange(B_ROWS)[None, :]).reshape(-1)
    bf = jnp.bfloat16
    t3a = np.stack([pick(cos_t)[ra], pick(sin_t)[ra]]).reshape(2, ROWS, 128, LANES).astype(bf)
    t3b = np.stack([pick(cos_t)[rb], pick(sin_t)[rb]]).reshape(2, ROWS * B_ROWS, LANES).astype(bf)
    t2 = np.stack([cos_t.T, sin_t.T]).reshape(2, ROWS, COLS, N_GRID).astype(bf)
    return t2, t3a, t3b


def body(y_h, wr_h, wc_h, gr_h, gc_h, vc, s_h, d_h, t2_h, t3a_h, t3b_h, out_ref,
         y, wr, wc, gr, gc, s_v, din, drow, dcol, dd, rt0, rt1, wd, lb0, lb1, la0, la1, lh, accb, acc, gbb, gb,
         hbufb, recvb, hbuf, recv,
         hs, hr, hrt, t2, t3a, t3b, ib, img, yrecv, ctmp,
         in_sem, tab_sem, send_sem, recv_sem, hsend_sem, hrecv_sem, ysend_sem, yrecv_sem):
    rts = (rt0, rt1)
    lefts_b = (lb0, lb1)
    lefts = (la0, la1)
    me = lax.axis_index('rows')
    cid = lax.axis_index('coil')
    nxt = lax.rem(me + 1, ROWS)
    prv = lax.rem(me + ROWS - 1, ROWS)
    other = 1 - cid

    ins = [pltpu.make_async_copy(a, b, in_sem.at[n]) for n, (a, b) in enumerate(
        ((gc_h, gc), (wc_h, wc), (gr_h, gr), (wr_h, wr), (y_h.at[0], y.at[0:8]), (y_h.at[1], y.at[8:16])))]
    for c in ins:
        c.start()
    tabs = [(t2_h.at[0], t2.at[:, 0]), (t2_h.at[1], t2.at[:, 1])]
    for g in range(3):
        src = slice(g * 128, g * 128 + 128)
        re = slice(g * 256, g * 256 + 128)
        im = slice(g * 256 + 128, g * 256 + 256)
        tabs += [
            (t3b_h.at[0, :, src], t3b.at[0, :, re]),
            (t3b_h.at[1, :, src], t3b.at[0, :, im]),
            (t3b_h.at[0, :, src], t3b.at[1, :, im]),
            (t3a_h.at[0, :, :, src], t3a.at[:, :, re]),
            (t3a_h.at[1, :, :, src], t3a.at[:, :, im]),
        ]
    tabs += [(s_h, s_v), (d_h, din)]
    tabs = [pltpu.make_async_copy(a, b, tab_sem.at[n]) for n, (a, b) in enumerate(tabs)]
    for c in tabs:
        c.start()

    barrier = pltpu.get_barrier_semaphore()
    for d in range(1, ROWS):
        pl.semaphore_signal(barrier, inc=1, device_id={'rows': lax.rem(me + d, ROWS)}, device_id_type=MESH)
    pl.semaphore_signal(barrier, inc=1, device_id={'coil': other}, device_id_type=MESH)
    for c in ins:
        c.wait()
    pl.semaphore_wait(barrier, 4)

    pieces = [(k * KC + o, 256) for k in range(NK) for o in range(0, KC, 256)]

    def build_wd(lo, groups):
        sl = pl.ds(lo, 256)
        keep = (lax.broadcasted_iota(jnp.int32, (1, 256), 1) + lo < vc[0]).astype(F32)
        first = gr[:, sl] - me * BLK
        taps = [(jnp.broadcast_to(first + (a - 2), (8, 256)), jnp.broadcast_to(wr[a:a + 1, sl] * keep, (8, 256)))
                for a in range(4)]
        ids = lax.broadcasted_iota(jnp.int32, (8, 1), 0)
        for n in groups:
            if n < 16:
                r = ids + (n * 8 + (B_ROWS if n * 8 >= B_FIRST else 0))
            elif n < 20:
                r = ids + (n * 8 - 128 + B_FIRST)
            else:
                r = jnp.where(ids == 0, BLK, ids - 3)
            for p, v in ((126, 16), (127, 32), (16, 158), (32, 159)):
                if p // 8 == n:
                    r = jnp.where(ids == p % 8, v, r)
            w = jnp.zeros((8, 256), F32)
            for t, v in taps:
                w = jnp.where(r == t, v, w)
            wd[n * 8:n * 8 + 8, sl] = w

    def build_rt(lo):
        sl = pl.ds(lo, 256)
        k, off = lo // HALF, lo % HALF
        col = gc[:, sl]
        taps = []
        for b in range(4):
            t = col + (b - 2)
            t = jnp.where(t < 0, t + N_GRID, jnp.where(t >= N_GRID, t - N_GRID, t))
            taps.append((jnp.broadcast_to(t, (16, 256)).astype(jnp.int16),
                         jnp.broadcast_to(wc[b:b + 1, sl], (16, 256)).astype(BF)))
        base = lax.broadcasted_iota(jnp.int16, (16, 256), 0)
        for n in range(N_GRID // 16):
            ids = base + jnp.int16(n * 16)
            w = jnp.zeros((16, 256), BF)
            for t, v in taps:
                w = jnp.where(ids == t, v, w)
            rts[k][n * 16:(n + 1) * 16, off:off + 256] = w

    def build_left_b(k, off):
        sl = pl.ds(k * KC + off, 256)
        w = wd[128:160, sl]
        for q in range(2):
            for c in range(NC):
                lo = q * 256 + c * 32
                lefts_b[k % 2][lo:lo + 32, off:off + 256] = (y[q * 8 + c:q * 8 + c + 1, sl] * w).astype(BF)

    def build_halo(lo):
        sl = pl.ds(lo, 256)
        for h in range(3):
            lh[h * 16:h * 16 + 16, sl] = (y[:, sl] * wd[160 + h:161 + h, sl]).astype(BF)

    def left_a_piece(c, lo):
        k, off = lo // HALF, lo % HALF
        sl = pl.ds(lo, 256)
        rows = [jnp.broadcast_to(y[pl.ds(q * 8 + c, 1), sl], (16, 256)) for q in range(2)]
        for n in range(8):
            w = wd[n * 16:n * 16 + 16, sl]
            for q, row in enumerate(rows):
                lefts[k][q * 128 + n * 16:q * 128 + n * 16 + 16, off:off + 256] = (row * w).astype(BF)

    def build_left_a(c, k):
        for off in range(0, HALF, 256):
            left_a_piece(c, k * HALF + off)

    def nt(a, b):
        return lax.dot_general(a, b, (((1,), (1,)), ((), ())), preferred_element_type=F32)

    def exchange(stage):
        if stage is None:
            src, dst, idx = hbufb, recvb, NC
        else:
            src, dst, idx = hbuf.at[stage], recv.at[stage], stage
        return [pltpu.make_async_remote_copy(
            src_ref=src.at[lax.rem(me + d, ROWS)], dst_ref=dst.at[me],
            send_sem=send_sem.at[idx, d - 1], recv_sem=recv_sem.at[idx, 3 - d],
            device_id={'rows': lax.rem(me + d, ROWS)}, device_id_type=MESH) for d in (1, 2, 3)]

    def received(stage):
        if stage is None:
            src, dst, idx = hbufb, recvb, NC
        else:
            src, dst, idx = hbuf.at[stage], recv.at[stage], stage
        return [pltpu.make_async_remote_copy(
            src_ref=src.at[0], dst_ref=dst.at[lax.rem(me + d, ROWS)],
            send_sem=send_sem.at[idx, d - 1], recv_sem=recv_sem.at[idx, d - 1],
            device_id={'rows': lax.rem(me + d, ROWS)}, device_id_type=MESH) for d in (1, 2, 3)]

    def transform(stage):
        g_ref, h_ref, r_ref = (gbb, hbufb, recvb) if stage is None else (gb, hbuf.at[stage], recv.at[stage])
        n = g_ref.shape[1] // 2
        for h in range(2):
            table = t2[2 * h:2 * h + 2].reshape(N_IMG, N_GRID)
            with_re = jnp.dot(table, g_ref[:, 0:n], preferred_element_type=F32) if n == 256 else None
            with_im = jnp.dot(table, g_ref[:, n:], preferred_element_type=F32) if n == 256 else None
            if n < 256:
                both = jnp.dot(table, g_ref[...], preferred_element_type=F32)
                with_re, with_im = both[:, 0:n], both[:, n:]
            for p in range(2):
                lo = p * 2 * COLS
                mid = lo + COLS
                end = mid + COLS
                h_ref[2 * h + p, 0:COLS] = (with_re[lo:mid] - with_im[mid:end]).astype(BF)
                h_ref[2 * h + p, COLS:] = (with_re[mid:end] + with_im[lo:mid]).astype(BF)

    def send(stage):
        h_ref, r_ref = (hbufb, recvb) if stage is None else (hbuf.at[stage], recv.at[stage])
        for c in exchange(stage):
            c.start()
        r_ref[me] = h_ref[me]

    halo = [None, None]
    for k in range(NK):
        for o in range(k * KC, (k + 1) * KC, 256):
            build_rt(o)
            build_wd(o, (20,))
            build_halo(o)
        off = (k % 2) * KC
        for h in range(2):
            part = nt(rts[k // 2][h * 320:h * 320 + 320, off:off + KC], lh[:, k * KC:(k + 1) * KC])
            halo[h] = part if k == 0 else halo[h] + part
    for o in range(0, KC, 256):
        build_wd(o, (16, 17, 18, 19))
        build_left_b(0, o)
    for h in range(2):
        hrt[h * 320:h * 320 + 320, 0:48] = halo[h]
    hs[...] = hrt[...].T[0:48]
    to_next = pltpu.make_async_remote_copy(
        src_ref=hs.at[0:16], dst_ref=hr.at[0:16], send_sem=hsend_sem.at[0], recv_sem=hrecv_sem.at[0],
        device_id={'rows': nxt}, device_id_type=MESH)
    to_prev = pltpu.make_async_remote_copy(
        src_ref=hs.at[16:48], dst_ref=hr.at[16:48], send_sem=hsend_sem.at[1], recv_sem=hrecv_sem.at[1],
        device_id={'rows': prv}, device_id_type=MESH)
    to_next.start()
    to_prev.start()
    for c in tabs:
        c.wait()

    for k in range(NK):
        off = (k % 2) * KC
        for q in range(2):
            cs = slice(q * 256, q * 256 + 256)
            part = nt(rts[k // 2][:, off:off + KC], lefts_b[k % 2][cs, :])
            if k == 0:
                accb[:, cs] = part
            elif k + 1 < NK:
                accb[:, cs] += part
            else:
                gbb[:, cs] = (accb[:, cs] + part).astype(BF)
        if k >= NK // 2:
            for o in range((k - NK // 2) * KC, (k - NK // 2 + 1) * KC, 256):
                build_wd(o, range(16))
                left_a_piece(0, o)
        if k + 1 < NK:
            for o in range(0, KC, 256):
                build_wd((k + 1) * KC + o, (16, 17, 18, 19))
                build_left_b(k + 1, o)
    for g in range(3):
        t3b[1, :, g * 256:g * 256 + 128] = -t3b[0, :, g * 256 + 128:g * 256 + 256]
    drow[:, 0:N_IMG] = din[...].reshape(1, N_IMG)
    dcol[...] = jnp.broadcast_to(din[...].reshape(1, N_IMG), (8, N_IMG)).T
    dd[...] = dcol[pl.ds(pl.multiple_of(me * COLS, COLS), COLS), 0:1] * drow[:, pl.ds(pl.multiple_of(cid * 128, 128), 256)]
    img[...] = jnp.zeros_like(img)
    transform(None)
    send(None)

    def spread_head(c, first=False):
        for h in range(2):
            rows = slice(h * 320, h * 320 + 320)
            acc[rows, :] = nt(rts[0][rows, :], lefts[0][...])
        for lo in range(HALF, SLOTS, 256):
            if first:
                build_wd(lo, range(16))
            left_a_piece(c, lo)

    lane = lax.broadcasted_iota(jnp.int32, (1, 128), 1)
    edge = (lane == 0) | (lane == 16) | (lane == 32)

    def spread_tail(c):
        for h in range(2):
            rows = slice(h * 320, h * 320 + 320)
            part = nt(rts[1][rows, :], lefts[1][...])
            for q in range(2):
                cs = slice(q * 128, q * 128 + 128)
                rolled = pltpu.roll(hrt[rows, :], 128 - (q * 8 + c), 1)
                gb[rows, cs] = (acc[rows, cs] + part[:, cs] + jnp.where(edge, rolled, 0.0)).astype(BF)

    def image_first():
        for c in received(None):
            c.wait_recv()
        for c in range(NC):
            blocks = [recvb[p, b * COLS:(b + 1) * COLS, c * 32:c * 32 + 32] for b in range(2) for p in range(ROWS)]
            lhs = jnp.concatenate(blocks, axis=1)
            ib[c] = jnp.dot(lhs, t3b[...].reshape(256, 2 * LANES), preferred_element_type=F32)

    def image_wait(c):
        for x in received(c):
            x.wait_recv()

    def image_coil(c):
        lhs = jnp.concatenate([recv[c, p] for p in range(ROWS)], axis=1)
        for g in range(3):
            lanes = slice(g * 256, g * 256 + 256)
            tot = jnp.dot(lhs, t3a[:, :, lanes].reshape(4 * 128, 256), preferred_element_type=F32)
            re = ib[c, :, g * 256:g * 256 + 128] + (tot[0:COLS, 0:128] - tot[COLS:, 128:])
            im = ib[c, :, g * 256 + 128:g * 256 + 256] + (tot[0:COLS, 128:] + tot[COLS:, 0:128])
            n = min(128, N_IMG - g * 128)
            at = slice(g * 128, g * 128 + n)
            sr = s_v[0, c, :, at]
            si = s_v[1, c, :, at]
            img[0, :, at] += sr * re[:, 0:n] + si * im[:, 0:n]
            img[1, :, at] += sr * im[:, 0:n] - si * re[:, 0:n]

    spread_head(0, True)

    @pl.loop(0, LAG)
    def _(c):
        @pl.when(c == 0)
        def _():
            to_next.wait()
            to_prev.wait()
            hrt[...] = jnp.concatenate([hr[...], jnp.zeros((80, N_GRID), F32)], axis=0).T

        spread_tail(c)
        build_left_a(c + 1, 0)
        transform(c)
        spread_head(c + 1)
        send(c)

    image_first()

    @pl.loop(LAG, NC - 1)
    def _(c):
        image_wait(c - LAG)
        spread_tail(c)
        build_left_a(c + 1, 0)
        image_coil(c - LAG)
        transform(c)
        spread_head(c + 1)
        send(c)

    spread_tail(NC - 1)
    transform(NC - 1)
    send(NC - 1)

    @pl.loop(NC - 1 - LAG, NC)
    def _(c):
        image_wait(c)
        image_coil(c)

    sends = [pltpu.make_async_remote_copy(
        src_ref=img.at[e, :, pl.ds(pl.multiple_of(other * 128, 128), 256)], dst_ref=yrecv.at[e],
        send_sem=ysend_sem.at[e], recv_sem=yrecv_sem.at[e],
        device_id={'coil': other}, device_id_type=MESH) for e in range(2)]
    for c in sends:
        c.start()
    for e in range(2):
        sends[e].wait()
        total = (img[e, :, pl.ds(pl.multiple_of(cid * 128, 128), 256)] + yrecv[e]) * dd[...]
        ctmp[e] = total.T
        out_ref[e] = ctmp[e, pl.ds(pl.multiple_of(cid * 32, 32), BLK), :]
    for stage in [None] + list(range(NC)):
        for c in received(stage):
            c.wait_send()


def solution(mesh):
    t2c, t3ac, t3bc = constants()

    def local_part(kspace, weight_row, weight_col, grid_row, grid_col, valid_count, coil_maps, deapod):
        any_spec = pl.BlockSpec(memory_space=pl.ANY)
        dma = pltpu.SemaphoreType.DMA
        return pl.pallas_call(
            body,
            out_shape=pltpu.VMEM((2, BLK, COLS), F32),
            in_specs=[any_spec] * 5 + [pl.BlockSpec(memory_space=pltpu.SMEM)] + [any_spec] * 5,
            out_specs=pl.BlockSpec(memory_space=pltpu.VMEM),
            scratch_shapes=[
                pltpu.VMEM((2 * NC, SLOTS), F32),
                pltpu.VMEM((4, SLOTS), F32),
                pltpu.VMEM((4, SLOTS), F32),
                pltpu.VMEM((1, SLOTS), jnp.int32),
                pltpu.VMEM((1, SLOTS), jnp.int32),
                pltpu.VMEM((2, NC, COLS, N_IMG), F32),
                pltpu.VMEM((N_IMG,), F32),
                pltpu.VMEM((1, LANES), F32),
                pltpu.VMEM((N_IMG, 8), F32),
                pltpu.VMEM((COLS, 256), F32),
                pltpu.VMEM((N_GRID, HALF), BF),
                pltpu.VMEM((N_GRID, HALF), BF),
                pltpu.VMEM((168, SLOTS), F32),
                pltpu.VMEM((512, KC), BF),
                pltpu.VMEM((512, KC), BF),
                pltpu.VMEM((256, HALF), BF),
                pltpu.VMEM((256, HALF), BF),
                pltpu.VMEM((48, SLOTS), BF),
                pltpu.VMEM((N_GRID, 512), F32),
                pltpu.VMEM((N_GRID, 256), F32),
                pltpu.VMEM((N_GRID, 512), BF),
                pltpu.VMEM((N_GRID, 256), BF),
                pltpu.VMEM((ROWS, 2 * COLS, 256), BF),
                pltpu.VMEM((ROWS, 2 * COLS, 256), BF),
                pltpu.VMEM((NC, ROWS, 2 * COLS, 128), BF),
                pltpu.VMEM((NC, ROWS, 2 * COLS, 128), BF),
                pltpu.VMEM((48, N_GRID), F32),
                pltpu.VMEM((48, N_GRID), F32),
                pltpu.VMEM((N_GRID, 128), F32),
                pltpu.VMEM((ROWS, 2, COLS, N_GRID), BF),
                pltpu.VMEM((ROWS, 128, 2 * LANES), BF),
                pltpu.VMEM((2, ROWS * B_ROWS, 2 * LANES), BF),
                pltpu.VMEM((NC, COLS, 2 * LANES), F32),
                pltpu.VMEM((2, COLS, LANES), F32),
                pltpu.VMEM((2, COLS, 256), F32),
                pltpu.VMEM((2, 256, COLS), F32),
                dma((6,)), dma((19,)), dma((9, 3)), dma((9, 3)), dma((2,)), dma((2,)), dma((2,)), dma((2,)),
            ],
            compiler_params=pltpu.CompilerParams(collective_id=0, has_side_effects=True, vmem_limit_bytes=60 * 1024 * 1024),
            name='nufft_adjoint',
        )(kspace, weight_row, weight_col, grid_row.reshape(1, SLOTS), grid_col.reshape(1, SLOTS), valid_count,
          jnp.swapaxes(coil_maps, 2, 3), deapod, jnp.asarray(t2c), jnp.asarray(t3ac), jnp.asarray(t3bc))

    spec_samples = P(None, 'coil', ('slab', 'rows'))
    spec_weights = P(None, ('slab', 'rows'))
    spec_index = P(('slab', 'rows'))
    return jax.shard_map(local_part, mesh=mesh, in_specs=(spec_samples, spec_weights, spec_weights, spec_index, spec_index, spec_index, P(None, 'coil', 'slab', 'rows'), P()), out_specs=P(None, ('slab', 'coil'), 'rows'), check_vma=False)
```

time: 43.9 us -> 44.5 us (1.014)
  Pallas kernels: 42.4 us -> 43 us
    pallas_call x1, Pallas kernels: 42.4 us -> 43 us  [local_part(): pl.pallas_call(body, out_shape=pltpu.VMEM((2, BLK, COLS), F32), in_specs=...]
where the time goes in v3:
time: 44.5 us; the launch traced here: 44.4 us
  Pallas kernels  43 us (97%)
  local copies, waits for them, and re-layouts  0.67 us (2%)
  between operations  0.66 us (1%)
    pallas_call x1, Pallas kernels, local_part(): pl.pallas_call(body, out_shape=pltpu.VMEM((2, BLK, COLS), F32), in_specs=...  43 us

profile of v3, /device:TPU:0, one launch (start us, length us, event | category | flops | bytes accessed | tf_op | source)
XLA Modules:
  0.0 44.4 jit_solution(1170515074074784561)
XLA Ops:
  0.7 43.0 %nufft_adjoint.1 = f32[2,160,80]{2,1,0:T(8,128)S(1)} custom-call(f32[2,8,5120]{2,1,0:T(8,128)} %y_h.1, f32[4,5120]{1,0:T(4,128)} %wr_h.1, f32[4,5120]{1,0:T(4,128)} %wc_h.1, s32[1,5120]{1,0:T(1,128)} %bitcast.4, s32[1,5120]{1,0:T(1,128)} %bitcast.5, s32[1]{0:T(128)S(6)} %copy.14.vc, f32[2,8,80,320]{3,2,1,0:T(8,128)} %bitcast.3, f32[320]{0:T(512)} %d_h.1, ...), custom_call_target="tpu_custom_call" | custom-call | tf_op jit(solution)/shard_map/nufft_adjoint/pallas_call | solution.py:377
  43.7 0.7 %copy.13 = f32[2,160,80]{2,1,0:T(8,128)} copy(f32[2,160,80]{2,1,0:T(8,128)S(1)} %nufft_adjoint.1) | data formatting | bytes 204800

commit v4 on v3

--- a/solution.py
+++ b/solution.py
@@ -59,7 +59,7 @@
 def body(y_h, wr_h, wc_h, gr_h, gc_h, vc, s_h, d_h, t2_h, t3a_h, t3b_h, out_ref,
          y, wr, wc, gr, gc, s_v, din, drow, dcol, dd, rt0, rt1, wd, lb0, lb1, la0, la1, lh, accb, acc, gbb, gb,
          hbufb, recvb, hbuf, recv,
-         hs, hr, hrt, t2, t3a, t3b, ib, img, yrecv, ctmp,
+         hs, hr, hrt, t2, t3a, t3b, ib, img, ysend, yrecv,
          in_sem, tab_sem, send_sem, recv_sem, hsend_sem, hrecv_sem, ysend_sem, yrecv_sem):
     rts = (rt0, rt1)
     lefts_b = (lb0, lb1)
@@ -213,21 +213,40 @@
             c.start()
         r_ref[me] = h_ref[me]
 
-    halo = [None, None]
-    for k in range(NK):
-        for o in range(k * KC, (k + 1) * KC, 256):
-            build_rt(o)
-            build_wd(o, (20,))
-            build_halo(o)
-        off = (k % 2) * KC
-        for h in range(2):
-            part = nt(rts[k // 2][h * 320:h * 320 + 320, off:off + KC], lh[:, k * KC:(k + 1) * KC])
-            halo[h] = part if k == 0 else halo[h] + part
-    for o in range(0, KC, 256):
-        build_wd(o, (16, 17, 18, 19))
-        build_left_b(0, o)
+    parts = [(0, 0, 256), (0, 256, KC - 256)] + [(k, 0, KC) for k in range(1, NK)]
+
+    def build_first(k, off, size):
+        for o in range(off, off + size, 256):
+            build_rt(k * KC + o)
+            build_wd(k * KC + o, (16, 17, 18, 19, 20))
+            build_left_b(k, o)
+            build_halo(k * KC + o)
+
+    def first_stage(n):
+        k, off, size = parts[n]
+        lo = (k % 2) * KC + off
+        for q in range(2):
+            cs = slice(q * 256, q * 256 + 256)
+            part = nt(rts[k // 2][:, lo:lo + size], lefts_b[k % 2][cs, off:off + size])
+            if n == 0:
+                accb[:, cs] = part
+            elif n + 1 < len(parts):
+                accb[:, cs] += part
+            else:
+                gbb[:, cs] = (accb[:, cs] + part).astype(BF)
+
+    build_first(*parts[0])
+    for n in range(len(parts) - 1):
+        first_stage(n)
+        build_first(*parts[n + 1])
+
     for h in range(2):
-        hrt[h * 320:h * 320 + 320, 0:48] = halo[h]
+        rows = slice(h * 320, h * 320 + 320)
+        halo = nt(rts[0][rows, :], lh[:, 0:HALF]) + nt(rts[1][rows, :], lh[:, HALF:])
+        hrt[rows, 0:48] = halo
+    for lo in range(0, HALF, 256):
+        build_wd(lo, range(16))
+        left_a_piece(0, lo)
     hs[...] = hrt[...].T[0:48]
     to_next = pltpu.make_async_remote_copy(
         src_ref=hs.at[0:16], dst_ref=hr.at[0:16], send_sem=hsend_sem.at[0], recv_sem=hrecv_sem.at[0],
@@ -240,30 +259,13 @@
     for c in tabs:
         c.wait()
 
-    for k in range(NK):
-        off = (k % 2) * KC
-        for q in range(2):
-            cs = slice(q * 256, q * 256 + 256)
-            part = nt(rts[k // 2][:, off:off + KC], lefts_b[k % 2][cs, :])
-            if k == 0:
-                accb[:, cs] = part
-            elif k + 1 < NK:
-                accb[:, cs] += part
-            else:
-                gbb[:, cs] = (accb[:, cs] + part).astype(BF)
-        if k >= NK // 2:
-            for o in range((k - NK // 2) * KC, (k - NK // 2 + 1) * KC, 256):
-                build_wd(o, range(16))
-                left_a_piece(0, o)
-        if k + 1 < NK:
-            for o in range(0, KC, 256):
-                build_wd((k + 1) * KC + o, (16, 17, 18, 19))
-                build_left_b(k + 1, o)
+    first_stage(len(parts) - 1)
     for g in range(3):
         t3b[1, :, g * 256:g * 256 + 128] = -t3b[0, :, g * 256 + 128:g * 256 + 256]
-    drow[:, 0:N_IMG] = din[...].reshape(1, N_IMG)
+    drow[...] = din[...].reshape(1, N_IMG)
     dcol[...] = jnp.broadcast_to(din[...].reshape(1, N_IMG), (8, N_IMG)).T
-    dd[...] = dcol[pl.ds(pl.multiple_of(me * COLS, COLS), COLS), 0:1] * drow[:, pl.ds(pl.multiple_of(cid * 128, 128), 256)]
+    mine = jnp.where(cid == 0, drow[:, 0:BLK], drow[:, BLK:])
+    dd[...] = dcol[pl.ds(pl.multiple_of(me * COLS, COLS), COLS), 0:1] * mine
     img[...] = jnp.zeros_like(img)
     transform(None)
     send(None)
@@ -352,17 +354,18 @@
         image_wait(c)
         image_coil(c)
 
-    sends = [pltpu.make_async_remote_copy(
-        src_ref=img.at[e, :, pl.ds(pl.multiple_of(other * 128, 128), 256)], dst_ref=yrecv.at[e],
-        send_sem=ysend_sem.at[e], recv_sem=yrecv_sem.at[e],
-        device_id={'coil': other}, device_id_type=MESH) for e in range(2)]
-    for c in sends:
-        c.start()
+    halves = [jnp.where(cid == 0, img[e, :, BLK:N_IMG], img[e, :, 0:BLK]) for e in range(2)]
+    ysend[...] = jnp.concatenate([x[r:r + COLS // 2] for x in halves for r in (0, COLS // 2)], axis=1)
+    swap = pltpu.make_async_remote_copy(
+        src_ref=ysend, dst_ref=yrecv, send_sem=ysend_sem, recv_sem=yrecv_sem,
+        device_id={'coil': other}, device_id_type=MESH)
+    swap.start()
+    swap.wait()
     for e in range(2):
-        sends[e].wait()
-        total = (img[e, :, pl.ds(pl.multiple_of(cid * 128, 128), 256)] + yrecv[e]) * dd[...]
-        ctmp[e] = total.T
-        out_ref[e] = ctmp[e, pl.ds(pl.multiple_of(cid * 32, 32), BLK), :]
+        lo = e * 2 * BLK
+        theirs = jnp.concatenate([yrecv[:, lo:lo + BLK], yrecv[:, lo + BLK:lo + 2 * BLK]], axis=0)
+        total = (jnp.where(cid == 0, img[e, :, 0:BLK], img[e, :, BLK:N_IMG]) + theirs) * dd[...]
+        out_ref[e] = total.T
     for stage in [None] + list(range(NC)):
         for c in received(stage):
             c.wait_send()
@@ -387,9 +390,9 @@
                 pltpu.VMEM((1, SLOTS), jnp.int32),
                 pltpu.VMEM((2, NC, COLS, N_IMG), F32),
                 pltpu.VMEM((N_IMG,), F32),
-                pltpu.VMEM((1, LANES), F32),
+                pltpu.VMEM((1, N_IMG), F32),
                 pltpu.VMEM((N_IMG, 8), F32),
-                pltpu.VMEM((COLS, 256), F32),
+                pltpu.VMEM((COLS, BLK), F32),
                 pltpu.VMEM((N_GRID, HALF), BF),
                 pltpu.VMEM((N_GRID, HALF), BF),
                 pltpu.VMEM((168, SLOTS), F32),
@@ -413,10 +416,10 @@
                 pltpu.VMEM((ROWS, 128, 2 * LANES), BF),
                 pltpu.VMEM((2, ROWS * B_ROWS, 2 * LANES), BF),
                 pltpu.VMEM((NC, COLS, 2 * LANES), F32),
-                pltpu.VMEM((2, COLS, LANES), F32),
-                pltpu.VMEM((2, COLS, 256), F32),
-                pltpu.VMEM((2, 256, COLS), F32),
-                dma((6,)), dma((19,)), dma((9, 3)), dma((9, 3)), dma((2,)), dma((2,)), dma((2,)), dma((2,)),
+                pltpu.VMEM((2, COLS, N_IMG), F32),
+                pltpu.VMEM((COLS // 2, 4 * BLK), F32),
+                pltpu.VMEM((COLS // 2, 4 * BLK), F32),
+                dma((6,)), dma((19,)), dma((9, 3)), dma((9, 3)), dma((2,)), dma((2,)), dma, dma,
             ],
             compiler_params=pltpu.CompilerParams(collective_id=0, has_side_effects=True, vmem_limit_bytes=60 * 1024 * 1024),
             name='nufft_adjoint',

time: 44.5 us -> 43.4 us (0.975)
  Pallas kernels: 43 us -> 41.9 us
    pallas_call x1, Pallas kernels: 43 us -> 41.9 us  [local_part(): pl.pallas_call(body, out_shape=pltpu.VMEM((2, BLK, COLS), F32), in_specs=...]
where the time goes in v4:
time: 43.4 us; the launch traced here: 43.3 us
  Pallas kernels  41.9 us (97%)
  local copies, waits for them, and re-layouts  0.67 us (2%)
  between operations  0.66 us (2%)
    pallas_call x1, Pallas kernels, local_part(): pl.pallas_call(body, out_shape=pltpu.VMEM((2, BLK, COLS), F32), in_specs=...  41.9 us

profile of v4, /device:TPU:0, one launch (start us, length us, event | category | flops | bytes accessed | tf_op | source)
XLA Modules:
  0.0 43.3 jit_solution(11526132259273280654)
XLA Ops:
  0.7 41.9 %nufft_adjoint.1 = f32[2,160,80]{2,1,0:T(8,128)S(1)} custom-call(f32[2,8,5120]{2,1,0:T(8,128)} %y_h.1, f32[4,5120]{1,0:T(4,128)} %wr_h.1, f32[4,5120]{1,0:T(4,128)} %wc_h.1, s32[1,5120]{1,0:T(1,128)} %bitcast.4, s32[1,5120]{1,0:T(1,128)} %bitcast.5, s32[1]{0:T(128)S(6)} %copy.14.vc, f32[2,8,80,320]{3,2,1,0:T(8,128)} %bitcast.3, f32[320]{0:T(512)} %d_h.1, ...), custom_call_target="tpu_custom_call" | custom-call | tf_op jit(solution)/shard_map/nufft_adjoint/pallas_call | solution.py:380
  42.6 0.7 %copy.13 = f32[2,160,80]{2,1,0:T(8,128)} copy(f32[2,160,80]{2,1,0:T(8,128)S(1)} %nufft_adjoint.1) | data formatting | bytes 204800

commit v5 on v4

--- a/solution.py
+++ b/solution.py
@@ -23,6 +23,7 @@
 LANES = 384
 HALF = SLOTS // 2
 LAG = 3
+W = 256
 B_FIRST = 64
 B_ROWS = 32
 
@@ -88,24 +89,21 @@
         ]
     tabs += [(s_h, s_v), (d_h, din)]
     tabs = [pltpu.make_async_copy(a, b, tab_sem.at[n]) for n, (a, b) in enumerate(tabs)]
-    for c in tabs:
-        c.start()
-
     barrier = pltpu.get_barrier_semaphore()
     for d in range(1, ROWS):
         pl.semaphore_signal(barrier, inc=1, device_id={'rows': lax.rem(me + d, ROWS)}, device_id_type=MESH)
     pl.semaphore_signal(barrier, inc=1, device_id={'coil': other}, device_id_type=MESH)
     for c in ins:
         c.wait()
+    for c in tabs:
+        c.start()
     pl.semaphore_wait(barrier, 4)
 
-    pieces = [(k * KC + o, 256) for k in range(NK) for o in range(0, KC, 256)]
-
     def build_wd(lo, groups):
-        sl = pl.ds(lo, 256)
-        keep = (lax.broadcasted_iota(jnp.int32, (1, 256), 1) + lo < vc[0]).astype(F32)
+        sl = pl.ds(lo, W)
+        keep = (lax.broadcasted_iota(jnp.int32, (1, W), 1) + lo < vc[0]).astype(F32)
         first = gr[:, sl] - me * BLK
-        taps = [(jnp.broadcast_to(first + (a - 2), (8, 256)), jnp.broadcast_to(wr[a:a + 1, sl] * keep, (8, 256)))
+        taps = [(jnp.broadcast_to(first + (a - 2), (8, W)), jnp.broadcast_to(wr[a:a + 1, sl] * keep, (8, W)))
                 for a in range(4)]
         ids = lax.broadcasted_iota(jnp.int32, (8, 1), 0)
         for n in groups:
@@ -118,53 +116,53 @@
             for p, v in ((126, 16), (127, 32), (16, 158), (32, 159)):
                 if p // 8 == n:
                     r = jnp.where(ids == p % 8, v, r)
-            w = jnp.zeros((8, 256), F32)
+            w = jnp.zeros((8, W), F32)
             for t, v in taps:
                 w = jnp.where(r == t, v, w)
             wd[n * 8:n * 8 + 8, sl] = w
 
     def build_rt(lo):
-        sl = pl.ds(lo, 256)
+        sl = pl.ds(lo, W)
         k, off = lo // HALF, lo % HALF
         col = gc[:, sl]
         taps = []
         for b in range(4):
             t = col + (b - 2)
             t = jnp.where(t < 0, t + N_GRID, jnp.where(t >= N_GRID, t - N_GRID, t))
-            taps.append((jnp.broadcast_to(t, (16, 256)).astype(jnp.int16),
-                         jnp.broadcast_to(wc[b:b + 1, sl], (16, 256)).astype(BF)))
-        base = lax.broadcasted_iota(jnp.int16, (16, 256), 0)
+            taps.append((jnp.broadcast_to(t, (16, W)).astype(jnp.int16),
+                         jnp.broadcast_to(wc[b:b + 1, sl], (16, W)).astype(BF)))
+        base = lax.broadcasted_iota(jnp.int16, (16, W), 0)
         for n in range(N_GRID // 16):
             ids = base + jnp.int16(n * 16)
-            w = jnp.zeros((16, 256), BF)
+            w = jnp.zeros((16, W), BF)
             for t, v in taps:
                 w = jnp.where(ids == t, v, w)
-            rts[k][n * 16:(n + 1) * 16, off:off + 256] = w
+            rts[k][n * 16:(n + 1) * 16, off:off + W] = w
 
     def build_left_b(k, off):
-        sl = pl.ds(k * KC + off, 256)
+        sl = pl.ds(k * KC + off, W)
         w = wd[128:160, sl]
         for q in range(2):
             for c in range(NC):
                 lo = q * 256 + c * 32
-                lefts_b[k % 2][lo:lo + 32, off:off + 256] = (y[q * 8 + c:q * 8 + c + 1, sl] * w).astype(BF)
+                lefts_b[k % 2][lo:lo + 32, off:off + W] = (y[q * 8 + c:q * 8 + c + 1, sl] * w).astype(BF)
 
     def build_halo(lo):
-        sl = pl.ds(lo, 256)
+        sl = pl.ds(lo, W)
         for h in range(3):
             lh[h * 16:h * 16 + 16, sl] = (y[:, sl] * wd[160 + h:161 + h, sl]).astype(BF)
 
     def left_a_piece(c, lo):
         k, off = lo // HALF, lo % HALF
-        sl = pl.ds(lo, 256)
-        rows = [jnp.broadcast_to(y[pl.ds(q * 8 + c, 1), sl], (16, 256)) for q in range(2)]
+        sl = pl.ds(lo, W)
+        rows = [jnp.broadcast_to(y[pl.ds(q * 8 + c, 1), sl], (16, W)) for q in range(2)]
         for n in range(8):
             w = wd[n * 16:n * 16 + 16, sl]
             for q, row in enumerate(rows):
-                lefts[k][q * 128 + n * 16:q * 128 + n * 16 + 16, off:off + 256] = (row * w).astype(BF)
+                lefts[k][q * 128 + n * 16:q * 128 + n * 16 + 16, off:off + W] = (row * w).astype(BF)
 
     def build_left_a(c, k):
-        for off in range(0, HALF, 256):
+        for off in range(0, HALF, W):
             left_a_piece(c, k * HALF + off)
 
     def nt(a, b):
@@ -216,7 +214,7 @@
     parts = [(0, 0, 256), (0, 256, KC - 256)] + [(k, 0, KC) for k in range(1, NK)]
 
     def build_first(k, off, size):
-        for o in range(off, off + size, 256):
+        for o in range(off, off + size, W):
             build_rt(k * KC + o)
             build_wd(k * KC + o, (16, 17, 18, 19, 20))
             build_left_b(k, o)
@@ -235,16 +233,21 @@
             else:
                 gbb[:, cs] = (accb[:, cs] + part).astype(BF)
 
+    def halo(k):
+        lo = (k % 2) * KC
+        for h in range(2):
+            rows = slice(h * 320, h * 320 + 320)
+            part = nt(rts[k // 2][rows, lo:lo + KC], lh[:, k * KC:(k + 1) * KC])
+            hrt[rows, 0:48] = part if k == 0 else hrt[rows, 0:48] + part
+
     build_first(*parts[0])
     for n in range(len(parts) - 1):
         first_stage(n)
+        if n > 0:
+            halo(parts[n][0])
         build_first(*parts[n + 1])
-
-    for h in range(2):
-        rows = slice(h * 320, h * 320 + 320)
-        halo = nt(rts[0][rows, :], lh[:, 0:HALF]) + nt(rts[1][rows, :], lh[:, HALF:])
-        hrt[rows, 0:48] = halo
-    for lo in range(0, HALF, 256):
+    halo(NK - 1)
+    for lo in range(0, HALF, W):
         build_wd(lo, range(16))
         left_a_piece(0, lo)
     hs[...] = hrt[...].T[0:48]
@@ -274,7 +277,7 @@
         for h in range(2):
             rows = slice(h * 320, h * 320 + 320)
             acc[rows, :] = nt(rts[0][rows, :], lefts[0][...])
-        for lo in range(HALF, SLOTS, 256):
+        for lo in range(HALF, SLOTS, W):
             if first:
                 build_wd(lo, range(16))
             left_a_piece(c, lo)
@@ -335,7 +338,7 @@
 
     image_first()
 
-    @pl.loop(LAG, NC - 1)
+    @pl.loop(LAG, NC - 2)
     def _(c):
         image_wait(c - LAG)
         spread_tail(c)
@@ -345,9 +348,17 @@
         spread_head(c + 1)
         send(c)
 
-    spread_tail(NC - 1)
-    transform(NC - 1)
-    send(NC - 1)
+    c = NC - 2
+    image_wait(c - LAG)
+    spread_tail(c)
+    build_left_a(c + 1, 0)
+    image_coil(c - LAG)
+    transform(c)
+    send(c)
+    spread_head(c + 1)
+    spread_tail(c + 1)
+    transform(c + 1)
+    send(c + 1)
 
     @pl.loop(NC - 1 - LAG, NC)
     def _(c):

time: 43.4 us -> 42 us (0.968)
  Pallas kernels: 41.9 us -> 40.6 us
    pallas_call x1, Pallas kernels: 41.9 us -> 40.6 us  [local_part(): pl.pallas_call(body, out_shape=pltpu.VMEM((2, BLK, COLS), F32), in_specs=...]
where the time goes in v5:
time: 42 us; the launch traced here: 41.9 us
  Pallas kernels  40.6 us (97%)
  local copies, waits for them, and re-layouts  0.67 us (2%)
  between operations  0.66 us (2%)
    pallas_call x1, Pallas kernels, local_part(): pl.pallas_call(body, out_shape=pltpu.VMEM((2, BLK, COLS), F32), in_specs=...  40.6 us

profile of v5, /device:TPU:0, one launch (start us, length us, event | category | flops | bytes accessed | tf_op | source)
XLA Modules:
  0.0 41.9 jit_solution(3802066880723628698)
XLA Ops:
  0.7 40.6 %nufft_adjoint.1 = f32[2,160,80]{2,1,0:T(8,128)S(1)} custom-call(f32[2,8,5120]{2,1,0:T(8,128)} %y_h.1, f32[4,5120]{1,0:T(4,128)} %wr_h.1, f32[4,5120]{1,0:T(4,128)} %wc_h.1, s32[1,5120]{1,0:T(1,128)} %bitcast.4, s32[1,5120]{1,0:T(1,128)} %bitcast.5, s32[1]{0:T(128)S(6)} %copy.14.vc, f32[2,8,80,320]{3,2,1,0:T(8,128)} %bitcast.3, f32[320]{0:T(512)} %d_h.1, ...), custom_call_target="tpu_custom_call" | custom-call | tf_op jit(solution)/shard_map/nufft_adjoint/pallas_call | solution.py:391
  41.2 0.7 %copy.13 = f32[2,160,80]{2,1,0:T(8,128)} copy(f32[2,160,80]{2,1,0:T(8,128)S(1)} %nufft_adjoint.1) | data formatting | bytes 204800

commit v6 on v5

--- a/solution.py
+++ b/solution.py
@@ -102,41 +102,54 @@
     def build_wd(lo, groups):
         sl = pl.ds(lo, W)
         keep = (lax.broadcasted_iota(jnp.int32, (1, W), 1) + lo < vc[0]).astype(F32)
-        first = gr[:, sl] - me * BLK
-        taps = [(jnp.broadcast_to(first + (a - 2), (8, W)), jnp.broadcast_to(wr[a:a + 1, sl] * keep, (8, W)))
-                for a in range(4)]
-        ids = lax.broadcasted_iota(jnp.int32, (8, 1), 0)
+        start = gr[:, sl] - me * BLK - 2
+        ids = lax.broadcasted_iota(jnp.int32, (8, W), 0)
+        taps = [jnp.broadcast_to(wr[a:a + 1, sl] * keep, (8, W)) for a in range(4)]
+        group = jnp.broadcast_to(lax.shift_right_arithmetic(start + 8, 3) - 1, (8, W))
+        within = jnp.broadcast_to(start + 8 & 7, (8, W))
+        head = jnp.zeros((8, W), F32)
+        over = jnp.zeros((8, W), F32)
+        for a in range(4):
+            head = jnp.where(ids == within + a, taps[a], head)
+            over = jnp.where(ids == within + (a - 8), taps[a], over)
+
+        def rows_of(n):
+            return jnp.where(group == n, head, jnp.where(group == n - 1, over, 0.0))
+
         for n in groups:
             if n < 16:
-                r = ids + (n * 8 + (B_ROWS if n * 8 >= B_FIRST else 0))
+                w = rows_of(n + (B_ROWS // 8 if n * 8 >= B_FIRST else 0))
             elif n < 20:
-                r = ids + (n * 8 - 128 + B_FIRST)
+                w = rows_of(n - 16 + B_FIRST // 8)
             else:
-                r = jnp.where(ids == 0, BLK, ids - 3)
-            for p, v in ((126, 16), (127, 32), (16, 158), (32, 159)):
-                if p // 8 == n:
-                    r = jnp.where(ids == p % 8, v, r)
-            w = jnp.zeros((8, W), F32)
-            for t, v in taps:
-                w = jnp.where(r == t, v, w)
+                w = jnp.where(ids == 0, rows_of(BLK // 8), pltpu.roll(rows_of(-1), 3, 0))
             wd[n * 8:n * 8 + 8, sl] = w
+        if 15 in groups:
+            for p, v in ((126, 16), (127, 32)):
+                one, two = wd[p:p + 1, sl], wd[v:v + 1, sl]
+                wd[p:p + 1, sl] = two
+                wd[v:v + 1, sl] = one
 
     def build_rt(lo):
         sl = pl.ds(lo, W)
         k, off = lo // HALF, lo % HALF
-        col = gc[:, sl]
-        taps = []
+        start = gc[:, sl] - 2
+        start = jnp.where(start < 0, start + N_GRID, start)
+        group = lax.shift_right_arithmetic(start, 4)
+        after = jnp.where(group == N_GRID // 16 - 1, 0, group + 1)
+        group = jnp.broadcast_to(group, (16, W)).astype(jnp.int16)
+        after = jnp.broadcast_to(after, (16, W)).astype(jnp.int16)
+        within = jnp.broadcast_to(start & 15, (16, W))
+        ids = lax.broadcasted_iota(jnp.int16, (16, W), 0)
+        head = jnp.zeros((16, W), BF)
+        over = jnp.zeros((16, W), BF)
         for b in range(4):
-            t = col + (b - 2)
-            t = jnp.where(t < 0, t + N_GRID, jnp.where(t >= N_GRID, t - N_GRID, t))
-            taps.append((jnp.broadcast_to(t, (16, W)).astype(jnp.int16),
-                         jnp.broadcast_to(wc[b:b + 1, sl], (16, W)).astype(BF)))
-        base = lax.broadcasted_iota(jnp.int16, (16, W), 0)
+            v = jnp.broadcast_to(wc[b:b + 1, sl], (16, W)).astype(BF)
+            head = jnp.where(ids == (within + b).astype(jnp.int16), v, head)
+            over = jnp.where(ids == (within + (b - 16)).astype(jnp.int16), v, over)
+        zero = jnp.zeros((16, W), BF)
         for n in range(N_GRID // 16):
-            ids = base + jnp.int16(n * 16)
-            w = jnp.zeros((16, W), BF)
-            for t, v in taps:
-                w = jnp.where(ids == t, v, w)
+            w = jnp.where(group == jnp.int16(n), head, jnp.where(after == jnp.int16(n), over, zero))
             rts[k][n * 16:(n + 1) * 16, off:off + W] = w
 
     def build_left_b(k, off):
@@ -295,8 +308,6 @@
                 gb[rows, cs] = (acc[rows, cs] + part[:, cs] + jnp.where(edge, rolled, 0.0)).astype(BF)
 
     def image_first():
-        for c in received(None):
-            c.wait_recv()
         for c in range(NC):
             blocks = [recvb[p, b * COLS:(b + 1) * COLS, c * 32:c * 32 + 32] for b in range(2) for p in range(ROWS)]
             lhs = jnp.concatenate(blocks, axis=1)
@@ -322,7 +333,7 @@
 
     spread_head(0, True)
 
-    @pl.loop(0, LAG)
+    @pl.loop(0, LAG - 1)
     def _(c):
         @pl.when(c == 0)
         def _():
@@ -336,7 +347,15 @@
         spread_head(c + 1)
         send(c)
 
+    for c in received(None):
+        c.wait_recv()
+    c = LAG - 1
+    spread_tail(c)
+    build_left_a(c + 1, 0)
     image_first()
+    transform(c)
+    spread_head(c + 1)
+    send(c)
 
     @pl.loop(LAG, NC - 2)
     def _(c):

time: 42 us -> 40.9 us (0.974)
  Pallas kernels: 40.6 us -> 39.5 us
    pallas_call x1, Pallas kernels: 40.6 us -> 39.5 us  [local_part(): pl.pallas_call(body, out_shape=pltpu.VMEM((2, BLK, COLS), F32), in_specs=...]
where the time goes in v6:
time: 40.9 us; the launch traced here: 40.8 us
  Pallas kernels  39.5 us (97%)
  local copies, waits for them, and re-layouts  0.67 us (2%)
  between operations  0.66 us (2%)
    pallas_call x1, Pallas kernels, local_part(): pl.pallas_call(body, out_shape=pltpu.VMEM((2, BLK, COLS), F32), in_specs=...  39.5 us

profile of v6, /device:TPU:0, one launch (start us, length us, event | category | flops | bytes accessed | tf_op | source)
XLA Modules:
  0.0 40.8 jit_solution(7735011505438735593)
XLA Ops:
  0.7 39.5 %nufft_adjoint.1 = f32[2,160,80]{2,1,0:T(8,128)S(1)} custom-call(f32[2,8,5120]{2,1,0:T(8,128)} %y_h.1, f32[4,5120]{1,0:T(4,128)} %wr_h.1, f32[4,5120]{1,0:T(4,128)} %wc_h.1, s32[1,5120]{1,0:T(1,128)} %bitcast.4, s32[1,5120]{1,0:T(1,128)} %bitcast.5, s32[1]{0:T(128)S(6)} %copy.14.vc, f32[2,8,80,320]{3,2,1,0:T(8,128)} %bitcast.3, f32[320]{0:T(512)} %d_h.1, ...), custom_call_target="tpu_custom_call" | custom-call | tf_op jit(solution)/shard_map/nufft_adjoint/pallas_call | solution.py:410
  40.1 0.7 %copy.13 = f32[2,160,80]{2,1,0:T(8,128)} copy(f32[2,160,80]{2,1,0:T(8,128)S(1)} %nufft_adjoint.1) | data formatting | bytes 204800

commit v7 on v6

--- a/solution.py
+++ b/solution.py
@@ -23,6 +23,7 @@
 LANES = 384
 HALF = SLOTS // 2
 LAG = 3
+LATE = 2
 W = 256
 B_FIRST = 64
 B_ROWS = 32
@@ -60,7 +61,7 @@
 def body(y_h, wr_h, wc_h, gr_h, gc_h, vc, s_h, d_h, t2_h, t3a_h, t3b_h, out_ref,
          y, wr, wc, gr, gc, s_v, din, drow, dcol, dd, rt0, rt1, wd, lb0, lb1, la0, la1, lh, accb, acc, gbb, gb,
          hbufb, recvb, hbuf, recv,
-         hs, hr, hrt, t2, t3a, t3b, ib, img, ysend, yrecv,
+         hs, hr, hrt, t2, t3a, t3b, ib, img, own, ysend, yrecv,
          in_sem, tab_sem, send_sem, recv_sem, hsend_sem, hrecv_sem, ysend_sem, yrecv_sem):
     rts = (rt0, rt1)
     lefts_b = (lb0, lb1)
@@ -255,7 +256,8 @@
 
     build_first(*parts[0])
     for n in range(len(parts) - 1):
-        first_stage(n)
+        if n + LATE < len(parts):
+            first_stage(n)
         if n > 0:
             halo(parts[n][0])
         build_first(*parts[n + 1])
@@ -275,7 +277,8 @@
     for c in tabs:
         c.wait()
 
-    first_stage(len(parts) - 1)
+    for n in range(len(parts) - LATE, len(parts)):
+        first_stage(n)
     for g in range(3):
         t3b[1, :, g * 256:g * 256 + 128] = -t3b[0, :, g * 256 + 128:g * 256 + 256]
     drow[...] = din[...].reshape(1, N_IMG)
@@ -333,7 +336,7 @@
 
     spread_head(0, True)
 
-    @pl.loop(0, LAG - 1)
+    @pl.loop(0, LAG)
     def _(c):
         @pl.when(c == 0)
         def _():
@@ -349,15 +352,17 @@
 
     for c in received(None):
         c.wait_recv()
-    c = LAG - 1
+    c = LAG
+    image_wait(c - LAG)
     spread_tail(c)
     build_left_a(c + 1, 0)
     image_first()
+    image_coil(c - LAG)
     transform(c)
     spread_head(c + 1)
     send(c)
 
-    @pl.loop(LAG, NC - 2)
+    @pl.loop(LAG + 1, NC - 2)
     def _(c):
         image_wait(c - LAG)
         spread_tail(c)
@@ -390,15 +395,16 @@
         src_ref=ysend, dst_ref=yrecv, send_sem=ysend_sem, recv_sem=yrecv_sem,
         device_id={'coil': other}, device_id_type=MESH)
     swap.start()
+    for e in range(2):
+        own[e] = jnp.where(cid == 0, img[e, :, 0:BLK], img[e, :, BLK:N_IMG])
+    for stage in [None] + list(range(NC)):
+        for c in received(stage):
+            c.wait_send()
     swap.wait()
     for e in range(2):
         lo = e * 2 * BLK
         theirs = jnp.concatenate([yrecv[:, lo:lo + BLK], yrecv[:, lo + BLK:lo + 2 * BLK]], axis=0)
-        total = (jnp.where(cid == 0, img[e, :, 0:BLK], img[e, :, BLK:N_IMG]) + theirs) * dd[...]
-        out_ref[e] = total.T
-    for stage in [None] + list(range(NC)):
-        for c in received(stage):
-            c.wait_send()
+        out_ref[e] = ((own[e] + theirs) * dd[...]).T
 
 
 def solution(mesh):
@@ -447,6 +453,7 @@
                 pltpu.VMEM((2, ROWS * B_ROWS, 2 * LANES), BF),
                 pltpu.VMEM((NC, COLS, 2 * LANES), F32),
                 pltpu.VMEM((2, COLS, N_IMG), F32),
+                pltpu.VMEM((2, COLS, BLK), F32),
                 pltpu.VMEM((COLS // 2, 4 * BLK), F32),
                 pltpu.VMEM((COLS // 2, 4 * BLK), F32),
                 dma((6,)), dma((19,)), dma((9, 3)), dma((9, 3)), dma((2,)), dma((2,)), dma, dma,

time: 40.9 us -> 41 us (level)
  no operation moved by 1% of the time
where the time goes in v7:
time: 41 us; the launch traced here: 40.9 us
  Pallas kernels  39.5 us (96%)
  local copies, waits for them, and re-layouts  0.67 us (2%)
  between operations  0.66 us (2%)
    pallas_call x1, Pallas kernels, local_part(): pl.pallas_call(body, out_shape=pltpu.VMEM((2, BLK, COLS), F32), in_specs=...  39.5 us

profile of v7, /device:TPU:0, one launch (start us, length us, event | category | flops | bytes accessed | tf_op | source)
XLA Modules:
  0.0 40.9 jit_solution(15304293186286663380)
XLA Ops:
  0.7 39.5 %nufft_adjoint.1 = f32[2,160,80]{2,1,0:T(8,128)S(1)} custom-call(f32[2,8,5120]{2,1,0:T(8,128)} %y_h.1, f32[4,5120]{1,0:T(4,128)} %wr_h.1, f32[4,5120]{1,0:T(4,128)} %wc_h.1, s32[1,5120]{1,0:T(1,128)} %bitcast.4, s32[1,5120]{1,0:T(1,128)} %bitcast.5, s32[1]{0:T(128)S(6)} %copy.14.vc, f32[2,8,80,320]{3,2,1,0:T(8,128)} %bitcast.3, f32[320]{0:T(512)} %d_h.1, ...), custom_call_target="tpu_custom_call" | custom-call | tf_op jit(solution)/shard_map/nufft_adjoint/pallas_call | solution.py:416
  40.2 0.7 %copy.13 = f32[2,160,80]{2,1,0:T(8,128)} copy(f32[2,160,80]{2,1,0:T(8,128)S(1)} %nufft_adjoint.1) | data formatting | bytes 204800

commit v8 on v7

--- a/solution.py
+++ b/solution.py
@@ -22,8 +22,7 @@
 NK = SLOTS // KC
 LANES = 384
 HALF = SLOTS // 2
-LAG = 3
-LATE = 2
+LATE = 1
 W = 256
 B_FIRST = 64
 B_ROWS = 32
@@ -316,10 +315,6 @@
             lhs = jnp.concatenate(blocks, axis=1)
             ib[c] = jnp.dot(lhs, t3b[...].reshape(256, 2 * LANES), preferred_element_type=F32)
 
-    def image_wait(c):
-        for x in received(c):
-            x.wait_recv()
-
     def image_coil(c):
         lhs = jnp.concatenate([recv[c, p] for p in range(ROWS)], axis=1)
         for g in range(3):
@@ -336,7 +331,7 @@
 
     spread_head(0, True)
 
-    @pl.loop(0, LAG)
+    @pl.loop(0, NC - 2)
     def _(c):
         @pl.when(c == 0)
         def _():
@@ -350,33 +345,9 @@
         spread_head(c + 1)
         send(c)
 
-    for c in received(None):
-        c.wait_recv()
-    c = LAG
-    image_wait(c - LAG)
+    c = NC - 2
     spread_tail(c)
     build_left_a(c + 1, 0)
-    image_first()
-    image_coil(c - LAG)
-    transform(c)
-    spread_head(c + 1)
-    send(c)
-
-    @pl.loop(LAG + 1, NC - 2)
-    def _(c):
-        image_wait(c - LAG)
-        spread_tail(c)
-        build_left_a(c + 1, 0)
-        image_coil(c - LAG)
-        transform(c)
-        spread_head(c + 1)
-        send(c)
-
-    c = NC - 2
-    image_wait(c - LAG)
-    spread_tail(c)
-    build_left_a(c + 1, 0)
-    image_coil(c - LAG)
     transform(c)
     send(c)
     spread_head(c + 1)
@@ -384,9 +355,14 @@
     transform(c + 1)
     send(c + 1)
 
-    @pl.loop(NC - 1 - LAG, NC)
+    for c in received(None):
+        c.wait_recv()
+    image_first()
+
+    @pl.loop(0, NC)
     def _(c):
-        image_wait(c)
+        for x in received(c):
+            x.wait_recv()
         image_coil(c)
 
     halves = [jnp.where(cid == 0, img[e, :, BLK:N_IMG], img[e, :, 0:BLK]) for e in range(2)]

time: 41 us -> 40.4 us (0.985)
  Pallas kernels: 39.5 us -> 38.9 us
    pallas_call x1, Pallas kernels: 39.5 us -> 38.9 us  [local_part(): pl.pallas_call(body, out_shape=pltpu.VMEM((2, BLK, COLS), F32), in_specs=...]
where the time goes in v8:
time: 40.4 us; the launch traced here: 40.2 us
  Pallas kernels  38.9 us (96%)
  local copies, waits for them, and re-layouts  0.67 us (2%)
  between operations  0.66 us (2%)
    pallas_call x1, Pallas kernels, local_part(): pl.pallas_call(body, out_shape=pltpu.VMEM((2, BLK, COLS), F32), in_specs=...  38.9 us

profile of v8, /device:TPU:0, one launch (start us, length us, event | category | flops | bytes accessed | tf_op | source)
XLA Modules:
  0.0 40.2 jit_solution(3978887466362524618)
XLA Ops:
  0.7 38.9 %nufft_adjoint.1 = f32[2,160,80]{2,1,0:T(8,128)S(1)} custom-call(f32[2,8,5120]{2,1,0:T(8,128)} %y_h.1, f32[4,5120]{1,0:T(4,128)} %wr_h.1, f32[4,5120]{1,0:T(4,128)} %wc_h.1, s32[1,5120]{1,0:T(1,128)} %bitcast.4, s32[1,5120]{1,0:T(1,128)} %bitcast.5, s32[1]{0:T(128)S(6)} %copy.14.vc, f32[2,8,80,320]{3,2,1,0:T(8,128)} %bitcast.3, f32[320]{0:T(512)} %d_h.1, ...), custom_call_target="tpu_custom_call" | custom-call | tf_op jit(solution)/shard_map/nufft_adjoint/pallas_call | solution.py:392
  39.6 0.7 %copy.13 = f32[2,160,80]{2,1,0:T(8,128)} copy(f32[2,160,80]{2,1,0:T(8,128)S(1)} %nufft_adjoint.1) | data formatting | bytes 204800

commit v9 on v8

--- a/solution.py
+++ b/solution.py
@@ -57,8 +57,8 @@
     return t2, t3a, t3b
 
 
-def body(y_h, wr_h, wc_h, gr_h, gc_h, vc, s_h, d_h, t2_h, t3a_h, t3b_h, out_ref,
-         y, wr, wc, gr, gc, s_v, din, drow, dcol, dd, rt0, rt1, wd, lb0, lb1, la0, la1, lh, accb, acc, gbb, gb,
+def body(y_h, wr_h, wc_h, gr_h, gc_h, vc_h, s_h, d_h, t2_h, t3a_h, t3b_h, out_ref,
+         y, wr, wc, gr, gc, vc, s_v, din, drow, dcol, dd, rt0, rt1, wd, lb0, lb1, la0, la1, lh, accb, acc, gbb, gb,
          hbufb, recvb, hbuf, recv,
          hs, hr, hrt, t2, t3a, t3b, ib, img, own, ysend, yrecv,
          in_sem, tab_sem, send_sem, recv_sem, hsend_sem, hrecv_sem, ysend_sem, yrecv_sem):
@@ -72,7 +72,7 @@
     other = 1 - cid
 
     ins = [pltpu.make_async_copy(a, b, in_sem.at[n]) for n, (a, b) in enumerate(
-        ((gc_h, gc), (wc_h, wc), (gr_h, gr), (wr_h, wr), (y_h.at[0], y.at[0:8]), (y_h.at[1], y.at[8:16])))]
+        ((gc_h, gc), (wc_h, wc), (vc_h, vc), (gr_h, gr), (wr_h, wr), (y_h.at[0], y.at[0:8]), (y_h.at[1], y.at[8:16])))]
     for c in ins:
         c.start()
     tabs = [(t2_h.at[0], t2.at[:, 0]), (t2_h.at[1], t2.at[:, 1])]
@@ -101,7 +101,7 @@
 
     def build_wd(lo, groups):
         sl = pl.ds(lo, W)
-        keep = (lax.broadcasted_iota(jnp.int32, (1, W), 1) + lo < vc[0]).astype(F32)
+        keep = (lax.broadcasted_iota(jnp.int32, (1, W), 1) + lo < vc[0, 0]).astype(F32)
         start = gr[:, sl] - me * BLK - 2
         ids = lax.broadcasted_iota(jnp.int32, (8, W), 0)
         taps = [jnp.broadcast_to(wr[a:a + 1, sl] * keep, (8, W)) for a in range(4)]
@@ -273,18 +273,11 @@
         device_id={'rows': prv}, device_id_type=MESH)
     to_next.start()
     to_prev.start()
-    for c in tabs:
+    for c in tabs[:2]:
         c.wait()
 
     for n in range(len(parts) - LATE, len(parts)):
         first_stage(n)
-    for g in range(3):
-        t3b[1, :, g * 256:g * 256 + 128] = -t3b[0, :, g * 256 + 128:g * 256 + 256]
-    drow[...] = din[...].reshape(1, N_IMG)
-    dcol[...] = jnp.broadcast_to(din[...].reshape(1, N_IMG), (8, N_IMG)).T
-    mine = jnp.where(cid == 0, drow[:, 0:BLK], drow[:, BLK:])
-    dd[...] = dcol[pl.ds(pl.multiple_of(me * COLS, COLS), COLS), 0:1] * mine
-    img[...] = jnp.zeros_like(img)
     transform(None)
     send(None)
 
@@ -355,6 +348,15 @@
     transform(c + 1)
     send(c + 1)
 
+    for c in tabs[2:]:
+        c.wait()
+    for g in range(3):
+        t3b[1, :, g * 256:g * 256 + 128] = -t3b[0, :, g * 256 + 128:g * 256 + 256]
+    drow[...] = din[...].reshape(1, N_IMG)
+    dcol[...] = jnp.broadcast_to(din[...].reshape(1, N_IMG), (8, N_IMG)).T
+    mine = jnp.where(cid == 0, drow[:, 0:BLK], drow[:, BLK:])
+    dd[...] = dcol[pl.ds(pl.multiple_of(me * COLS, COLS), COLS), 0:1] * mine
+    img[...] = jnp.zeros_like(img)
     for c in received(None):
         c.wait_recv()
     image_first()
@@ -392,7 +394,7 @@
         return pl.pallas_call(
             body,
             out_shape=pltpu.VMEM((2, BLK, COLS), F32),
-            in_specs=[any_spec] * 5 + [pl.BlockSpec(memory_space=pltpu.SMEM)] + [any_spec] * 5,
+            in_specs=[any_spec] * 5 + [pl.BlockSpec(memory_space=pltpu.HBM)] + [any_spec] * 5,
             out_specs=pl.BlockSpec(memory_space=pltpu.VMEM),
             scratch_shapes=[
                 pltpu.VMEM((2 * NC, SLOTS), F32),
@@ -400,6 +402,7 @@
                 pltpu.VMEM((4, SLOTS), F32),
                 pltpu.VMEM((1, SLOTS), jnp.int32),
                 pltpu.VMEM((1, SLOTS), jnp.int32),
+                pltpu.SMEM((1, 1), jnp.int32),
                 pltpu.VMEM((2, NC, COLS, N_IMG), F32),
                 pltpu.VMEM((N_IMG,), F32),
                 pltpu.VMEM((1, N_IMG), F32),
@@ -432,11 +435,11 @@
                 pltpu.VMEM((2, COLS, BLK), F32),
                 pltpu.VMEM((COLS // 2, 4 * BLK), F32),
                 pltpu.VMEM((COLS // 2, 4 * BLK), F32),
-                dma((6,)), dma((19,)), dma((9, 3)), dma((9, 3)), dma((2,)), dma((2,)), dma, dma,
+                dma((7,)), dma((19,)), dma((9, 3)), dma((9, 3)), dma((2,)), dma((2,)), dma, dma,
             ],
             compiler_params=pltpu.CompilerParams(collective_id=0, has_side_effects=True, vmem_limit_bytes=60 * 1024 * 1024),
             name='nufft_adjoint',
-        )(kspace, weight_row, weight_col, grid_row.reshape(1, SLOTS), grid_col.reshape(1, SLOTS), valid_count,
+        )(kspace, weight_row, weight_col, grid_row.reshape(1, SLOTS), grid_col.reshape(1, SLOTS), valid_count.reshape(1, 1),
           jnp.swapaxes(coil_maps, 2, 3), deapod, jnp.asarray(t2c), jnp.asarray(t3ac), jnp.asarray(t3bc))
 
     spec_samples = P(None, 'coil', ('slab', 'rows'))

time: 40.4 us -> 40.4 us (level)
  no operation moved by 1% of the time
where the time goes in v9:
time: 40.4 us; the launch traced here: 40.3 us
  Pallas kernels  39 us (97%)
  local copies, waits for them, and re-layouts  0.67 us (2%)
  between operations  0.66 us (2%)
    pallas_call x1, Pallas kernels, local_part(): pl.pallas_call(body, out_shape=pltpu.VMEM((2, BLK, COLS), F32), in_specs=...  39 us

profile of v9, /device:TPU:0, one launch (start us, length us, event | category | flops | bytes accessed | tf_op | source)
XLA Modules:
  0.0 40.3 jit_solution(354458954384762187)
XLA Ops:
  0.7 39.0 %nufft_adjoint.1 = f32[2,160,80]{2,1,0:T(8,128)S(1)} custom-call(f32[2,8,5120]{2,1,0:T(8,128)} %y_h.1, f32[4,5120]{1,0:T(4,128)} %wr_h.1, f32[4,5120]{1,0:T(4,128)} %wc_h.1, s32[1,5120]{1,0:T(1,128)} %bitcast.6, s32[1,5120]{1,0:T(1,128)} %bitcast.7, s32[1,1]{1,0:T(1,128)} %bitcast.4.vc_h, f32[2,8,80,320]{3,2,1,0:T(8,128)} %bitcast.5, f32[320]{0:T(512)} %d_h.1, ...), custom_call_target="tpu_custom_call" | custom-call | tf_op jit(solution)/shard_map/nufft_adjoint/pallas_call | solution.py:394
  39.7 0.7 %copy.13 = f32[2,160,80]{2,1,0:T(8,128)} copy(f32[2,160,80]{2,1,0:T(8,128)S(1)} %nufft_adjoint.1) | data formatting | bytes 204800

commit v10 on v8

--- a/solution.py
+++ b/solution.py
@@ -331,19 +331,21 @@
 
     spread_head(0, True)
 
-    @pl.loop(0, NC - 2)
-    def _(c):
-        @pl.when(c == 0)
-        def _():
-            to_next.wait()
-            to_prev.wait()
-            hrt[...] = jnp.concatenate([hr[...], jnp.zeros((80, N_GRID), F32)], axis=0).T
-
+    def advance(c):
         spread_tail(c)
         build_left_a(c + 1, 0)
         transform(c)
         spread_head(c + 1)
         send(c)
+
+    to_next.wait()
+    to_prev.wait()
+    hrt[...] = jnp.concatenate([hr[...], jnp.zeros((80, N_GRID), F32)], axis=0).T
+    advance(0)
+
+    @pl.loop(1, NC - 2)
+    def _(c):
+        advance(c)
 
     c = NC - 2
     spread_tail(c)
@@ -352,8 +354,27 @@
     send(c)
     spread_head(c + 1)
     spread_tail(c + 1)
-    transform(c + 1)
-    send(c + 1)
+    last = NC - 1
+    here = me // 2
+
+    def start(to):
+        d = lax.rem(to - me + ROWS, ROWS)
+        pltpu.make_async_remote_copy(
+            src_ref=hbuf.at[last, to], dst_ref=recv.at[last, me],
+            send_sem=send_sem.at[last, d - 1], recv_sem=recv_sem.at[last, 3 - d],
+            device_id={'rows': to}, device_id_type=MESH).start()
+
+    for chip in (1 - here, here):
+        for q in range(2):
+            to = 2 * chip + q
+            both = jnp.dot(t2[to].reshape(2 * COLS, N_GRID), gb[...], preferred_element_type=F32)
+            hbuf[last, to, 0:COLS] = (both[0:COLS, 0:128] - both[COLS:, 128:]).astype(BF)
+            hbuf[last, to, COLS:] = (both[COLS:, 0:128] + both[0:COLS, 128:]).astype(BF)
+        if chip is not here:
+            start(2 * chip)
+            start(2 * chip + 1)
+    start(2 * here + 1 - lax.rem(me, 2))
+    recv[last, me] = hbuf[last, me]
 
     for c in received(None):
         c.wait_recv()

time: 40.4 us -> 40.4 us (level)
  no operation moved by 1% of the time
where the time goes in v10:
time: 40.4 us; the launch traced here: 40.3 us
  Pallas kernels  39 us (97%)
  local copies, waits for them, and re-layouts  0.67 us (2%)
  between operations  0.66 us (2%)
    pallas_call x1, Pallas kernels, local_part(): pl.pallas_call(body, out_shape=pltpu.VMEM((2, BLK, COLS), F32), in_specs=...  39 us

profile of v10, /device:TPU:0, one launch (start us, length us, event | category | flops | bytes accessed | tf_op | source)
XLA Modules:
  0.0 40.3 jit_solution(6405348780830854871)
XLA Ops:
  0.7 39.0 %nufft_adjoint.1 = f32[2,160,80]{2,1,0:T(8,128)S(1)} custom-call(f32[2,8,5120]{2,1,0:T(8,128)} %y_h.1, f32[4,5120]{1,0:T(4,128)} %wr_h.1, f32[4,5120]{1,0:T(4,128)} %wc_h.1, s32[1,5120]{1,0:T(1,128)} %bitcast.4, s32[1,5120]{1,0:T(1,128)} %bitcast.5, s32[1]{0:T(128)S(6)} %copy.14.vc, f32[2,8,80,320]{3,2,1,0:T(8,128)} %bitcast.3, f32[320]{0:T(512)} %d_h.1, ...), custom_call_target="tpu_custom_call" | custom-call | tf_op jit(solution)/shard_map/nufft_adjoint/pallas_call | solution.py:413
  39.7 0.7 %copy.13 = f32[2,160,80]{2,1,0:T(8,128)} copy(f32[2,160,80]{2,1,0:T(8,128)S(1)} %nufft_adjoint.1) | data formatting | bytes 204800

commit v11 on v10

--- a/solution.py
+++ b/solution.py
@@ -22,7 +22,6 @@
 NK = SLOTS // KC
 LANES = 384
 HALF = SLOTS // 2
-LATE = 1
 W = 256
 B_FIRST = 64
 B_ROWS = 32
@@ -58,8 +57,7 @@
 
 
 def body(y_h, wr_h, wc_h, gr_h, gc_h, vc, s_h, d_h, t2_h, t3a_h, t3b_h, out_ref,
-         y, wr, wc, gr, gc, s_v, din, drow, dcol, dd, rt0, rt1, wd, lb0, lb1, la0, la1, lh, accb, acc, gbb, gb,
-         hbufb, recvb, hbuf, recv,
+         y, wr, wc, gr, gc, s_v, din, drow, dcol, dd, rt0, rt1, wd, lb0, lb1, la0, la1, lh, acc, gb, hbuf, recv,
          hs, hr, hrt, t2, t3a, t3b, ib, img, own, ysend, yrecv,
          in_sem, tab_sem, send_sem, recv_sem, hsend_sem, hrecv_sem, ysend_sem, yrecv_sem):
     rts = (rt0, rt1)
@@ -152,12 +150,13 @@
             w = jnp.where(group == jnp.int16(n), head, jnp.where(after == jnp.int16(n), over, zero))
             rts[k][n * 16:(n + 1) * 16, off:off + W] = w
 
-    def build_left_b(k, off):
+    def build_left_b(k, off, half):
         sl = pl.ds(k * KC + off, W)
         w = wd[128:160, sl]
         for q in range(2):
-            for c in range(NC):
-                lo = q * 256 + c * 32
+            for n in range(4):
+                c = half * 4 + n
+                lo = half * 256 + q * 128 + n * 32
                 lefts_b[k % 2][lo:lo + 32, off:off + W] = (y[q * 8 + c:q * 8 + c + 1, sl] * w).astype(BF)
 
     def build_halo(lo):
@@ -182,47 +181,33 @@
         return lax.dot_general(a, b, (((1,), (1,)), ((), ())), preferred_element_type=F32)
 
     def exchange(stage):
-        if stage is None:
-            src, dst, idx = hbufb, recvb, NC
-        else:
-            src, dst, idx = hbuf.at[stage], recv.at[stage], stage
+        src, dst, idx = hbuf.at[stage], recv.at[stage], stage
         return [pltpu.make_async_remote_copy(
             src_ref=src.at[lax.rem(me + d, ROWS)], dst_ref=dst.at[me],
             send_sem=send_sem.at[idx, d - 1], recv_sem=recv_sem.at[idx, 3 - d],
             device_id={'rows': lax.rem(me + d, ROWS)}, device_id_type=MESH) for d in (1, 2, 3)]
 
     def received(stage):
-        if stage is None:
-            src, dst, idx = hbufb, recvb, NC
-        else:
-            src, dst, idx = hbuf.at[stage], recv.at[stage], stage
+        src, dst, idx = hbuf.at[stage], recv.at[stage], stage
         return [pltpu.make_async_remote_copy(
             src_ref=src.at[0], dst_ref=dst.at[lax.rem(me + d, ROWS)],
             send_sem=send_sem.at[idx, d - 1], recv_sem=recv_sem.at[idx, d - 1],
             device_id={'rows': lax.rem(me + d, ROWS)}, device_id_type=MESH) for d in (1, 2, 3)]
 
     def transform(stage):
-        g_ref, h_ref, r_ref = (gbb, hbufb, recvb) if stage is None else (gb, hbuf.at[stage], recv.at[stage])
-        n = g_ref.shape[1] // 2
         for h in range(2):
-            table = t2[2 * h:2 * h + 2].reshape(N_IMG, N_GRID)
-            with_re = jnp.dot(table, g_ref[:, 0:n], preferred_element_type=F32) if n == 256 else None
-            with_im = jnp.dot(table, g_ref[:, n:], preferred_element_type=F32) if n == 256 else None
-            if n < 256:
-                both = jnp.dot(table, g_ref[...], preferred_element_type=F32)
-                with_re, with_im = both[:, 0:n], both[:, n:]
+            both = jnp.dot(t2[2 * h:2 * h + 2].reshape(N_IMG, N_GRID), gb[...], preferred_element_type=F32)
             for p in range(2):
                 lo = p * 2 * COLS
                 mid = lo + COLS
                 end = mid + COLS
-                h_ref[2 * h + p, 0:COLS] = (with_re[lo:mid] - with_im[mid:end]).astype(BF)
-                h_ref[2 * h + p, COLS:] = (with_re[mid:end] + with_im[lo:mid]).astype(BF)
+                hbuf[stage, 2 * h + p, 0:COLS] = (both[lo:mid, 0:128] - both[mid:end, 128:]).astype(BF)
+                hbuf[stage, 2 * h + p, COLS:] = (both[mid:end, 0:128] + both[lo:mid, 128:]).astype(BF)
 
     def send(stage):
-        h_ref, r_ref = (hbufb, recvb) if stage is None else (hbuf.at[stage], recv.at[stage])
         for c in exchange(stage):
             c.start()
-        r_ref[me] = h_ref[me]
+        recv[stage, me] = hbuf[stage, me]
 
     parts = [(0, 0, 256), (0, 256, KC - 256)] + [(k, 0, KC) for k in range(1, NK)]
 
@@ -230,40 +215,40 @@
         for o in range(off, off + size, W):
             build_rt(k * KC + o)
             build_wd(k * KC + o, (16, 17, 18, 19, 20))
-            build_left_b(k, o)
+            build_left_b(k, o, 0)
             build_halo(k * KC + o)
 
-    def first_stage(n):
-        k, off, size = parts[n]
+    def inner(k, off, size, half, begin, end):
         lo = (k % 2) * KC + off
-        for q in range(2):
-            cs = slice(q * 256, q * 256 + 256)
-            part = nt(rts[k // 2][:, lo:lo + size], lefts_b[k % 2][cs, off:off + size])
-            if n == 0:
-                accb[:, cs] = part
-            elif n + 1 < len(parts):
-                accb[:, cs] += part
-            else:
-                gbb[:, cs] = (accb[:, cs] + part).astype(BF)
-
-    def halo(k):
-        lo = (k % 2) * KC
         for h in range(2):
             rows = slice(h * 320, h * 320 + 320)
-            part = nt(rts[k // 2][rows, lo:lo + KC], lh[:, k * KC:(k + 1) * KC])
-            hrt[rows, 0:48] = part if k == 0 else hrt[rows, 0:48] + part
+            part = nt(rts[k // 2][rows, lo:lo + size], lefts_b[k % 2][half * 256:half * 256 + 256, off:off + size])
+            if begin:
+                acc[rows, :] = part
+            elif not end:
+                acc[rows, :] += part
+            else:
+                gb[rows, :] = (acc[rows, :] + part).astype(BF)
 
     build_first(*parts[0])
-    for n in range(len(parts) - 1):
-        if n + LATE < len(parts):
-            first_stage(n)
-        if n > 0:
-            halo(parts[n][0])
-        build_first(*parts[n + 1])
-    halo(NK - 1)
+    for n, part in enumerate(parts):
+        inner(*part, 0, n == 0, n + 1 == len(parts))
+        if n + 1 < len(parts):
+            build_first(*parts[n + 1])
+    for c in tabs:
+        c.wait()
+    transform(NC)
+    send(NC)
+
     for lo in range(0, HALF, W):
         build_wd(lo, range(16))
         left_a_piece(0, lo)
+    for k in range(2):
+        for o in range(0, KC, W):
+            build_left_b(k, o, 1)
+    for h in range(2):
+        rows = slice(h * 320, h * 320 + 320)
+        hrt[rows, 0:48] = nt(rts[0][rows, :], lh[:, 0:HALF]) + nt(rts[1][rows, :], lh[:, HALF:])
     hs[...] = hrt[...].T[0:48]
     to_next = pltpu.make_async_remote_copy(
         src_ref=hs.at[0:16], dst_ref=hr.at[0:16], send_sem=hsend_sem.at[0], recv_sem=hrecv_sem.at[0],
@@ -273,11 +258,11 @@
         device_id={'rows': prv}, device_id_type=MESH)
     to_next.start()
     to_prev.start()
-    for c in tabs:
-        c.wait()
-
-    for n in range(len(parts) - LATE, len(parts)):
-        first_stage(n)
+    for k in range(NK):
+        inner(k, 0, KC, 1, k == 0, k + 1 == NK)
+        if k + 2 < NK:
+            for o in range(0, KC, W):
+                build_left_b(k + 2, o, 1)
     for g in range(3):
         t3b[1, :, g * 256:g * 256 + 128] = -t3b[0, :, g * 256 + 128:g * 256 + 256]
     drow[...] = din[...].reshape(1, N_IMG)
@@ -285,8 +270,8 @@
     mine = jnp.where(cid == 0, drow[:, 0:BLK], drow[:, BLK:])
     dd[...] = dcol[pl.ds(pl.multiple_of(me * COLS, COLS), COLS), 0:1] * mine
     img[...] = jnp.zeros_like(img)
-    transform(None)
-    send(None)
+    transform(NC + 1)
+    send(NC + 1)
 
     def spread_head(c, first=False):
         for h in range(2):
@@ -311,7 +296,7 @@
 
     def image_first():
         for c in range(NC):
-            blocks = [recvb[p, b * COLS:(b + 1) * COLS, c * 32:c * 32 + 32] for b in range(2) for p in range(ROWS)]
+            blocks = [recv[NC + c // 4, p, b * COLS:(b + 1) * COLS, c % 4 * 32:c % 4 * 32 + 32] for b in range(2) for p in range(ROWS)]
             lhs = jnp.concatenate(blocks, axis=1)
             ib[c] = jnp.dot(lhs, t3b[...].reshape(256, 2 * LANES), preferred_element_type=F32)
 
@@ -376,8 +361,9 @@
     start(2 * here + 1 - lax.rem(me, 2))
     recv[last, me] = hbuf[last, me]
 
-    for c in received(None):
-        c.wait_recv()
+    for stage in (NC, NC + 1):
+        for c in received(stage):
+            c.wait_recv()
     image_first()
 
     @pl.loop(0, NC)
@@ -394,7 +380,7 @@
     swap.start()
     for e in range(2):
         own[e] = jnp.where(cid == 0, img[e, :, 0:BLK], img[e, :, BLK:N_IMG])
-    for stage in [None] + list(range(NC)):
+    for stage in range(NC + 2):
         for c in received(stage):
             c.wait_send()
     swap.wait()
@@ -434,14 +420,10 @@
                 pltpu.VMEM((256, HALF), BF),
                 pltpu.VMEM((256, HALF), BF),
                 pltpu.VMEM((48, SLOTS), BF),
-                pltpu.VMEM((N_GRID, 512), F32),
                 pltpu.VMEM((N_GRID, 256), F32),
-                pltpu.VMEM((N_GRID, 512), BF),
                 pltpu.VMEM((N_GRID, 256), BF),
-                pltpu.VMEM((ROWS, 2 * COLS, 256), BF),
-                pltpu.VMEM((ROWS, 2 * COLS, 256), BF),
-                pltpu.VMEM((NC, ROWS, 2 * COLS, 128), BF),
-                pltpu.VMEM((NC, ROWS, 2 * COLS, 128), BF),
+                pltpu.VMEM((NC + 2, ROWS, 2 * COLS, 128), BF),
+                pltpu.VMEM((NC + 2, ROWS, 2 * COLS, 128), BF),
                 pltpu.VMEM((48, N_GRID), F32),
                 pltpu.VMEM((48, N_GRID), F32),
                 pltpu.VMEM((N_GRID, 128), F32),
@@ -453,7 +435,7 @@
                 pltpu.VMEM((2, COLS, BLK), F32),
                 pltpu.VMEM((COLS // 2, 4 * BLK), F32),
                 pltpu.VMEM((COLS // 2, 4 * BLK), F32),
-                dma((6,)), dma((19,)), dma((9, 3)), dma((9, 3)), dma((2,)), dma((2,)), dma, dma,
+                dma((6,)), dma((19,)), dma((NC + 2, 3)), dma((NC + 2, 3)), dma((2,)), dma((2,)), dma, dma,
             ],
             compiler_params=pltpu.CompilerParams(collective_id=0, has_side_effects=True, vmem_limit_bytes=60 * 1024 * 1024),
             name='nufft_adjoint',

time: 40.4 us -> 40.7 us (level)
  no operation moved by 1% of the time
where the time goes in v11:
time: 40.7 us; the launch traced here: 40.6 us
  Pallas kernels  39.3 us (97%)
  local copies, waits for them, and re-layouts  0.67 us (2%)
  between operations  0.66 us (2%)
    pallas_call x1, Pallas kernels, local_part(): pl.pallas_call(body, out_shape=pltpu.VMEM((2, BLK, COLS), F32), in_specs=...  39.3 us

profile of v11, /device:TPU:0, one launch (start us, length us, event | category | flops | bytes accessed | tf_op | source)
XLA Modules:
  0.0 40.6 jit_solution(11386877329927278148)
XLA Ops:
  0.7 39.3 %nufft_adjoint.1 = f32[2,160,80]{2,1,0:T(8,128)S(1)} custom-call(f32[2,8,5120]{2,1,0:T(8,128)} %y_h.1, f32[4,5120]{1,0:T(4,128)} %wr_h.1, f32[4,5120]{1,0:T(4,128)} %wc_h.1, s32[1,5120]{1,0:T(1,128)} %bitcast.4, s32[1,5120]{1,0:T(1,128)} %bitcast.5, s32[1]{0:T(128)S(6)} %copy.14.vc, f32[2,8,80,320]{3,2,1,0:T(8,128)} %bitcast.3, f32[320]{0:T(512)} %d_h.1, ...), custom_call_target="tpu_custom_call" | custom-call | tf_op jit(solution)/shard_map/nufft_adjoint/pallas_call | solution.py:399
  40.0 0.7 %copy.13 = f32[2,160,80]{2,1,0:T(8,128)} copy(f32[2,160,80]{2,1,0:T(8,128)S(1)} %nufft_adjoint.1) | data formatting | bytes 204800

commit v12 on v10

--- a/solution.py
+++ b/solution.py
@@ -189,7 +189,7 @@
         return [pltpu.make_async_remote_copy(
             src_ref=src.at[lax.rem(me + d, ROWS)], dst_ref=dst.at[me],
             send_sem=send_sem.at[idx, d - 1], recv_sem=recv_sem.at[idx, 3 - d],
-            device_id={'rows': lax.rem(me + d, ROWS)}, device_id_type=MESH) for d in (1, 2, 3)]
+            device_id={'rows': lax.rem(me + d, ROWS)}, device_id_type=MESH) for d in (2, 1, 3)]
 
     def received(stage):
         if stage is None:
@@ -273,18 +273,11 @@
         device_id={'rows': prv}, device_id_type=MESH)
     to_next.start()
     to_prev.start()
-    for c in tabs:
+    for c in tabs[:2]:
         c.wait()
 
     for n in range(len(parts) - LATE, len(parts)):
         first_stage(n)
-    for g in range(3):
-        t3b[1, :, g * 256:g * 256 + 128] = -t3b[0, :, g * 256 + 128:g * 256 + 256]
-    drow[...] = din[...].reshape(1, N_IMG)
-    dcol[...] = jnp.broadcast_to(din[...].reshape(1, N_IMG), (8, N_IMG)).T
-    mine = jnp.where(cid == 0, drow[:, 0:BLK], drow[:, BLK:])
-    dd[...] = dcol[pl.ds(pl.multiple_of(me * COLS, COLS), COLS), 0:1] * mine
-    img[...] = jnp.zeros_like(img)
     transform(None)
     send(None)
 
@@ -376,6 +369,15 @@
     start(2 * here + 1 - lax.rem(me, 2))
     recv[last, me] = hbuf[last, me]
 
+    for c in tabs[2:]:
+        c.wait()
+    for g in range(3):
+        t3b[1, :, g * 256:g * 256 + 128] = -t3b[0, :, g * 256 + 128:g * 256 + 256]
+    drow[...] = din[...].reshape(1, N_IMG)
+    dcol[...] = jnp.broadcast_to(din[...].reshape(1, N_IMG), (8, N_IMG)).T
+    mine = jnp.where(cid == 0, drow[:, 0:BLK], drow[:, BLK:])
+    dd[...] = dcol[pl.ds(pl.multiple_of(me * COLS, COLS), COLS), 0:1] * mine
+    img[...] = jnp.zeros_like(img)
     for c in received(None):
         c.wait_recv()
     image_first()

time: 40.4 us -> 40.4 us (level)
  no operation moved by 1% of the time
where the time goes in v12:
time: 40.4 us; the launch traced here: 40.3 us
  Pallas kernels  39 us (97%)
  local copies, waits for them, and re-layouts  0.67 us (2%)
  between operations  0.66 us (2%)
    pallas_call x1, Pallas kernels, local_part(): pl.pallas_call(body, out_shape=pltpu.VMEM((2, BLK, COLS), F32), in_specs=...  39 us

profile of v12, /device:TPU:0, one launch (start us, length us, event | category | flops | bytes accessed | tf_op | source)
XLA Modules:
  0.0 40.3 jit_solution(15536413354180958726)
XLA Ops:
  0.7 39.0 %nufft_adjoint.1 = f32[2,160,80]{2,1,0:T(8,128)S(1)} custom-call(f32[2,8,5120]{2,1,0:T(8,128)} %y_h.1, f32[4,5120]{1,0:T(4,128)} %wr_h.1, f32[4,5120]{1,0:T(4,128)} %wc_h.1, s32[1,5120]{1,0:T(1,128)} %bitcast.4, s32[1,5120]{1,0:T(1,128)} %bitcast.5, s32[1]{0:T(128)S(6)} %copy.14.vc, f32[2,8,80,320]{3,2,1,0:T(8,128)} %bitcast.3, f32[320]{0:T(512)} %d_h.1, ...), custom_call_target="tpu_custom_call" | custom-call | tf_op jit(solution)/shard_map/nufft_adjoint/pallas_call | solution.py:415
  39.6 0.7 %copy.13 = f32[2,160,80]{2,1,0:T(8,128)} copy(f32[2,160,80]{2,1,0:T(8,128)S(1)} %nufft_adjoint.1) | data formatting | bytes 204800

commit v13 on v8

--- a/solution.py
+++ b/solution.py
@@ -189,7 +189,7 @@
         return [pltpu.make_async_remote_copy(
             src_ref=src.at[lax.rem(me + d, ROWS)], dst_ref=dst.at[me],
             send_sem=send_sem.at[idx, d - 1], recv_sem=recv_sem.at[idx, 3 - d],
-            device_id={'rows': lax.rem(me + d, ROWS)}, device_id_type=MESH) for d in (1, 2, 3)]
+            device_id={'rows': lax.rem(me + d, ROWS)}, device_id_type=MESH) for d in (2, 1, 3)]
 
     def received(stage):
         if stage is None:
@@ -331,19 +331,21 @@
 
     spread_head(0, True)
 
-    @pl.loop(0, NC - 2)
-    def _(c):
-        @pl.when(c == 0)
-        def _():
-            to_next.wait()
-            to_prev.wait()
-            hrt[...] = jnp.concatenate([hr[...], jnp.zeros((80, N_GRID), F32)], axis=0).T
-
+    def advance(c):
         spread_tail(c)
         build_left_a(c + 1, 0)
         transform(c)
         spread_head(c + 1)
         send(c)
+
+    to_next.wait()
+    to_prev.wait()
+    hrt[...] = jnp.concatenate([hr[...], jnp.zeros((80, N_GRID), F32)], axis=0).T
+    advance(0)
+
+    @pl.loop(1, NC - 2)
+    def _(c):
+        advance(c)
 
     c = NC - 2
     spread_tail(c)

time: 40.4 us -> 40.5 us (level)
  no operation moved by 1% of the time
where the time goes in v13:
time: 40.5 us; the launch traced here: 40.4 us
  Pallas kernels  39 us (96%)
  local copies, waits for them, and re-layouts  0.67 us (2%)
  between operations  0.66 us (2%)
    pallas_call x1, Pallas kernels, local_part(): pl.pallas_call(body, out_shape=pltpu.VMEM((2, BLK, COLS), F32), in_specs=...  39 us

profile of v13, /device:TPU:0, one launch (start us, length us, event | category | flops | bytes accessed | tf_op | source)
XLA Modules:
  0.0 40.4 jit_solution(6453898043078747370)
XLA Ops:
  0.7 39.0 %nufft_adjoint.1 = f32[2,160,80]{2,1,0:T(8,128)S(1)} custom-call(f32[2,8,5120]{2,1,0:T(8,128)} %y_h.1, f32[4,5120]{1,0:T(4,128)} %wr_h.1, f32[4,5120]{1,0:T(4,128)} %wc_h.1, s32[1,5120]{1,0:T(1,128)} %bitcast.4, s32[1,5120]{1,0:T(1,128)} %bitcast.5, s32[1]{0:T(128)S(6)} %copy.14.vc, f32[2,8,80,320]{3,2,1,0:T(8,128)} %bitcast.3, f32[320]{0:T(512)} %d_h.1, ...), custom_call_target="tpu_custom_call" | custom-call | tf_op jit(solution)/shard_map/nufft_adjoint/pallas_call | solution.py:394
  39.7 0.7 %copy.13 = f32[2,160,80]{2,1,0:T(8,128)} copy(f32[2,160,80]{2,1,0:T(8,128)S(1)} %nufft_adjoint.1) | data formatting | bytes 204800
